TPU v7x, 32 devices: a whole 2x2x4 slice. The times are simulated.
32 devices in a mesh: dom: 8 (over z, core), grp: 4 (over y, x).
Axes of the slice: x: 2, y: 2, z: 4, core: 2. Of those that a mesh axis runs over, the one named last changes fastest.
Arguments:
- fine_level_residual: float32 [3, 15, 4096], P(None, None, ('dom', 'grp')), may hold values from -6 to 6
- restriction_matrix: float32 [3, 15], replicated, may hold values from -1.5 to 1.5
- prolongation_matrix: float32 [15, 3], replicated, may hold values from -3.5 to 3.5
- block_inverse: bfloat16 [9, 9, 4096], P(None, None, 'dom')
- face_coupling: bfloat16 [3, 9, 9, 4096], P(None, None, None, 'dom'), may hold values from -1.75 to 1.75
- neighbours: int32 [3, 4096], P(None, 'dom'), may hold values from -512 to 512, as said below
Outputs:
- correction: float32 [3, 15, 4096], P(None, None, ('dom', 'grp'))
Inputs may be any that keep to these rules, and one draw needn't show every extreme that they name: `neighbours`: each entry is 0 or a nonzero offset d with |d| at most 512 such that e + d is another triangle of the grid.
All inputs are finite; a program needn't handle non-finite values.
Results may differ from a plain program's by a relative error of at most 0.0003.
Values sent between devices are 32-bit elements; how exact they have to be, the bound alone decides.
No kernel may reach another device: no remote copies, remote signals or barrier semaphores. Data moves between devices by JAX's collectives and lax.ppermute only.
A program may use at most 64 MiB of HBM per device.

v0:
```python
import jax
import jax.numpy as jnp
from jax import lax
from jax.sharding import PartitionSpec as P

SWEEPS = 6


damping = 0.8


def extended_2(block, sides, width):
    for axis, dim in sides:
        count = lax.axis_size(axis)
        forward = [(i, i + 1) for i in range(count - 1)]
        backward = [(target, source) for source, target in forward]
        low = lax.ppermute(
            lax.slice_in_dim(block, block.shape[dim] - width, None, axis=dim), axis, forward
        )
        high = lax.ppermute(lax.slice_in_dim(block, 0, width, axis=dim), axis, backward)
        block = jnp.concatenate([low, block, high], axis=dim)
    return block


def apply_inverse(block_inverse, remain):
    return jnp.sum(block_inverse.astype(jnp.float32) * remain[None, :, :], axis=1)


def later_sweep(
    current_iterate, coarse_forcing, block_inverse, face_coupling, neighbours, extended, anchor
):
    coupled = jnp.zeros_like(current_iterate)
    length = extended.shape[1]
    columns = jnp.arange(current_iterate.shape[1], dtype=jnp.int32)
    for face_index in range(3):
        offsets = neighbours[face_index]
        position = jnp.clip(columns + offsets + anchor, 0, length - 1)
        present = (offsets != 0).astype(jnp.float32)
        beside = extended[:, position] * present[None, :]
        coupled = coupled + jnp.sum(
            face_coupling[face_index].astype(jnp.float32) * beside[None, :, :], axis=1
        )
    update = apply_inverse(block_inverse, coarse_forcing - coupled)
    return (1.0 - damping) * current_iterate + damping * update


def local(
    fine_level_residual,
    restriction_matrix,
    prolongation_matrix,
    block_inverse,
    face_coupling,
    neighbours,
):
    element_width = fine_level_residual.shape[2]
    block_width = block_inverse.shape[2]
    local_rhs = jnp.einsum(
        "oc,acw->aow", restriction_matrix, fine_level_residual, precision=lax.Precision.HIGHEST
    )
    local_rhs = local_rhs.reshape(9, element_width)
    coarse_forcing = lax.all_gather(local_rhs, "grp", axis=1, tiled=True)
    current_iterate = damping * apply_inverse(block_inverse, coarse_forcing)
    for sweep_index in range(1, SWEEPS):
        extended = extended_2(current_iterate, (("dom", 1),), block_width)
        current_iterate = later_sweep(
            current_iterate,
            coarse_forcing,
            block_inverse,
            face_coupling,
            neighbours,
            extended,
            block_width,
        )
    owned_elements = lax.dynamic_slice_in_dim(
        current_iterate, lax.axis_index("grp") * element_width, element_width, 1
    )
    return jnp.einsum(
        "oc,dcz->doz",
        prolongation_matrix,
        owned_elements.reshape(3, 3, element_width),
        precision=lax.Precision.HIGHEST,
    )


def solution(mesh):
    placed = (
        P(None, None, ("dom", "grp")),
        P(),
        P(),
        P(None, None, "dom"),
        P(None, None, None, "dom"),
        P(None, "dom"),
    )
    return jax.shard_map(
        local, mesh=mesh, in_specs=placed, out_specs=P(None, None, ("dom", "grp")), check_vma=False
    )
```

profile of v0, /device:TPU:1, one launch (start us, length us, event | category | flops | bytes accessed | tf_op | source)
XLA Modules:
  0.0 74.5 jit_solution(7957785853049385496)
XLA Ops:
  0.0 0.7 copy-done
  0.7 0.8 %convolution_bitcast_fusion.1 = f32[3,3,128]{2,1,0:T(4,128)S(1)} fusion(f32[3,15,128]{2,1,0:T(8,128)S(1)} %copy-done, f32[3,15]{1,0:T(4,128)} %param.7), kind=kOutput, calls=%fused_computation.16 | convolution fusion | flops 207360 | bytes 27828 | tf_op jit(solution)/shard_map/oc,acw->aow/dot_general | solution.py:57
  1.6 7.1 %all_gather.3 = f32[9,512]{1,0:T(8,128)S(1)} all-gather(f32[9,128]{1,0:T(8,128)S(1)} %reshape.393), channel_id=1, replica_groups=mesh['dom'=8,'grp'=4] {'grp'}, dimensions={1}, use_global_device_ids=true | all-gather | bytes 23040 | tf_op jit(solution)/shard_map/all_gather | solution.py:61
  8.6 1.0 %fusion.15 = f32[9,512]{1,0:T(8,128)S(1)} fusion(bf16[9,9,512]{2,1,0:T(8,128)(2,1)} %param.9, f32[9,512]{1,0:T(8,128)S(1)} %all_gather.3), kind=kLoop, calls=%fused_computation.53 | loop fusion | flops 119808 | bytes 119808 | tf_op jit(solution)/shard_map/reduce_sum | solution.py:26
  9.7 5.8 %collective-permute-start = (f32[9,512]{1,0:T(8,128)S(1)}, f32[9,512]{1,0:T(8,128)S(1)}, u32[]{:S(2)}, u32[]{:S(2)}) collective-permute-start(f32[9,512]{1,0:T(8,128)S(1)} %broadcast_multiply_fusion), channel_id=1, source_target_pairs={{0,4},{4,8},{8,12},{12,16},{16,20},{20,24},{24,28},{1,5},{5,9},{9,... | collective-permute-start | bytes 55304 | tf_op jit(solution)/shard_map/ppermute | solution.py:17
  15.4 1.9 %collective-permute-start.1 = (f32[9,512]{1,0:T(8,128)S(1)}, f32[9,512]{1,0:T(8,128)S(1)}, u32[]{:S(2)}, u32[]{:S(2)}) collective-permute-start(f32[9,512]{1,0:T(8,128)S(1)} %broadcast_multiply_fusion), channel_id=1, source_target_pairs={{4,0},{8,4},{12,8},{16,12},{20,16},{24,20},{28,24},{5,1},{9,5},{13... | collective-permute-start | bytes 55304 | tf_op jit(solution)/shard_map/ppermute | solution.py:20
  17.4 0.4 fusion.30
  17.8 2.8 %collective-permute-done.1 = f32[9,512]{1,0:T(8,128)S(1)} collective-permute-done((f32[9,512]{1,0:T(8,128)S(1)}, f32[9,512]{1,0:T(8,128)S(1)}, u32[]{:S(2)}, u32[]{:S(2)}) %collective-permute-start.1) | collective-permute-done | bytes 18464 | tf_op jit(solution)/shard_map/ppermute | solution.py:20
  20.7 0.3 copy.43
  21.0 1.0 %gather_fusion = f32[512,9]{1,0:T(8,128)S(1)} fusion(f32[9,1536]{0,1:T(8,128)S(1)} %copy.43, s32[1024]{0:T(1024)S(1)} %pad_clamp_fusion.2), kind=kCustom, calls=%fused_computation | custom fusion | bytes 38912 | tf_op jit(solution)/shard_map/gather | solution.py:39
  22.0 0.1 multiply_bitcast_fusion.14
  22.1 0.1 copy.44
  22.3 1.0 %gather_fusion.1 = f32[512,9]{1,0:T(8,128)S(1)} fusion(f32[9,1536]{0,1:T(8,128)S(1)} %copy.43, s32[1024]{0:T(1024)S(1)} %pad_clamp_fusion.1), kind=kCustom, calls=%fused_computation.1 | custom fusion | bytes 38912 | tf_op jit(solution)/shard_map/gather | solution.py:39
  23.3 0.1 multiply_bitcast_fusion.13
  23.6 1.0 %gather_fusion.2 = f32[512,9]{1,0:T(8,128)S(1)} fusion(f32[9,1536]{0,1:T(8,128)S(1)} %copy.43, s32[1024]{0:T(1024)S(1)} %pad_clamp_fusion), kind=kCustom, calls=%fused_computation.2 | custom fusion | bytes 38912 | tf_op jit(solution)/shard_map/gather | solution.py:39
  24.6 0.1 multiply_bitcast_fusion.12
  24.9 0.1 fusion
  25.1 0.9 %copy-done.1 = bf16[9,9,512]{2,1,0:T(8,128)(2,1)S(1)} copy-done((bf16[9,9,512]{2,1,0:T(8,128)(2,1)S(1)}, bf16[9,9,512]{2,1,0:T(8,128)(2,1)}, u32[]{:S(2)}) %copy-start.1) | copy-done | bytes 82968
  26.1 1.9 %collective-permute-start.2 = (f32[9,512]{1,0:T(8,128)S(1)}, f32[9,512]{1,0:T(8,128)S(1)}, u32[]{:S(2)}, u32[]{:S(2)}) collective-permute-start(f32[9,512]{1,0:T(8,128)S(1)} %multiply_add_fusion.3), channel_id=1, source_target_pairs={{0,4},{4,8},{8,12},{12,16},{16,20},{20,24},{24,28},{1,5},{5,9},{9,... | collective-permute-start | bytes 55304 | tf_op jit(solution)/shard_map/ppermute | solution.py:17
  28.0 2.4 %collective-permute-start.3 = (f32[9,512]{1,0:T(8,128)S(1)}, f32[9,512]{1,0:T(8,128)S(1)}, u32[]{:S(2)}, u32[]{:S(2)}) collective-permute-start(f32[9,512]{1,0:T(8,128)S(1)} %multiply_add_fusion.3), channel_id=1, source_target_pairs={{4,0},{8,4},{12,8},{16,12},{20,16},{24,20},{28,24},{5,1},{9,5},{13... | collective-permute-start | bytes 55304 | tf_op jit(solution)/shard_map/ppermute | solution.py:20
  30.4 2.8 %collective-permute-done.3 = f32[9,512]{1,0:T(8,128)S(1)} collective-permute-done((f32[9,512]{1,0:T(8,128)S(1)}, f32[9,512]{1,0:T(8,128)S(1)}, u32[]{:S(2)}, u32[]{:S(2)}) %collective-permute-start.3) | collective-permute-done | bytes 18464 | tf_op jit(solution)/shard_map/ppermute | solution.py:20
  33.3 0.3 copy.51
  33.6 1.0 %gather_fusion.3 = f32[512,9]{1,0:T(8,128)S(1)} fusion(f32[9,1536]{0,1:T(8,128)S(1)} %copy.51, s32[1024]{0:T(1024)S(1)} %pad_clamp_fusion.2), kind=kCustom, calls=%fused_computation.3 | custom fusion | bytes 38912 | tf_op jit(solution)/shard_map/gather | solution.py:39
  34.6 1.0 %gather_fusion.4 = f32[512,9]{1,0:T(8,128)S(1)} fusion(f32[9,1536]{0,1:T(8,128)S(1)} %copy.51, s32[1024]{0:T(1024)S(1)} %pad_clamp_fusion.1), kind=kCustom, calls=%fused_computation.4 | custom fusion | bytes 38912 | tf_op jit(solution)/shard_map/gather | solution.py:39
  35.6 1.0 %gather_fusion.5 = f32[512,9]{1,0:T(8,128)S(1)} fusion(f32[9,1536]{0,1:T(8,128)S(1)} %copy.51, s32[1024]{0:T(1024)S(1)} %pad_clamp_fusion), kind=kCustom, calls=%fused_computation.5 | custom fusion | bytes 38912 | tf_op jit(solution)/shard_map/gather | solution.py:39
  36.7 0.1 multiply_bitcast_fusion.11
  37.0 0.1 multiply_bitcast_fusion.10
  37.4 0.1 multiply_bitcast_fusion.9
  37.8 1.9 %collective-permute-start.4 = (f32[9,512]{1,0:T(8,128)S(1)}, f32[9,512]{1,0:T(8,128)S(1)}, u32[]{:S(2)}, u32[]{:S(2)}) collective-permute-start(f32[9,512]{1,0:T(8,128)S(1)} %multiply_add_fusion.2), channel_id=1, source_target_pairs={{0,4},{4,8},{8,12},{12,16},{16,20},{20,24},{24,28},{1,5},{5,9},{9,... | collective-permute-start | bytes 55304 | tf_op jit(solution)/shard_map/ppermute | solution.py:17
  39.7 2.4 %collective-permute-start.5 = (f32[9,512]{1,0:T(8,128)S(1)}, f32[9,512]{1,0:T(8,128)S(1)}, u32[]{:S(2)}, u32[]{:S(2)}) collective-permute-start(f32[9,512]{1,0:T(8,128)S(1)} %multiply_add_fusion.2), channel_id=1, source_target_pairs={{4,0},{8,4},{12,8},{16,12},{20,16},{24,20},{28,24},{5,1},{9,5},{13... | collective-permute-start | bytes 55304 | tf_op jit(solution)/shard_map/ppermute | solution.py:20
  42.2 2.8 %collective-permute-done.5 = f32[9,512]{1,0:T(8,128)S(1)} collective-permute-done((f32[9,512]{1,0:T(8,128)S(1)}, f32[9,512]{1,0:T(8,128)S(1)}, u32[]{:S(2)}, u32[]{:S(2)}) %collective-permute-start.5) | collective-permute-done | bytes 18464 | tf_op jit(solution)/shard_map/ppermute | solution.py:20
  45.0 0.3 copy.57
  45.3 1.0 %gather_fusion.6 = f32[512,9]{1,0:T(8,128)S(1)} fusion(f32[9,1536]{0,1:T(8,128)S(1)} %copy.57, s32[1024]{0:T(1024)S(1)} %pad_clamp_fusion.2), kind=kCustom, calls=%fused_computation.6 | custom fusion | bytes 38912 | tf_op jit(solution)/shard_map/gather | solution.py:39
  46.3 1.0 %gather_fusion.7 = f32[512,9]{1,0:T(8,128)S(1)} fusion(f32[9,1536]{0,1:T(8,128)S(1)} %copy.57, s32[1024]{0:T(1024)S(1)} %pad_clamp_fusion.1), kind=kCustom, calls=%fused_computation.7 | custom fusion | bytes 38912 | tf_op jit(solution)/shard_map/gather | solution.py:39
  47.4 1.0 %gather_fusion.8 = f32[512,9]{1,0:T(8,128)S(1)} fusion(f32[9,1536]{0,1:T(8,128)S(1)} %copy.57, s32[1024]{0:T(1024)S(1)} %pad_clamp_fusion), kind=kCustom, calls=%fused_computation.8 | custom fusion | bytes 38912 | tf_op jit(solution)/shard_map/gather | solution.py:39
  48.4 0.1 multiply_bitcast_fusion.8
  48.8 0.1 multiply_bitcast_fusion.7
  49.1 0.1 multiply_bitcast_fusion.6
  49.2 0.1 copy.62
  49.5 1.9 %collective-permute-start.6 = (f32[9,512]{1,0:T(8,128)S(1)}, f32[9,512]{1,0:T(8,128)S(1)}, u32[]{:S(2)}, u32[]{:S(2)}) collective-permute-start(f32[9,512]{1,0:T(8,128)S(1)} %multiply_add_fusion.1), channel_id=1, source_target_pairs={{0,4},{4,8},{8,12},{12,16},{16,20},{20,24},{24,28},{1,5},{5,9},{9,... | collective-permute-start | bytes 55304 | tf_op jit(solution)/shard_map/ppermute | solution.py:17
  51.5 2.4 %collective-permute-start.7 = (f32[9,512]{1,0:T(8,128)S(1)}, f32[9,512]{1,0:T(8,128)S(1)}, u32[]{:S(2)}, u32[]{:S(2)}) collective-permute-start(f32[9,512]{1,0:T(8,128)S(1)} %multiply_add_fusion.1), channel_id=1, source_target_pairs={{4,0},{8,4},{12,8},{16,12},{20,16},{24,20},{28,24},{5,1},{9,5},{13... | collective-permute-start | bytes 55304 | tf_op jit(solution)/shard_map/ppermute | solution.py:20
  53.9 2.8 %collective-permute-done.7 = f32[9,512]{1,0:T(8,128)S(1)} collective-permute-done((f32[9,512]{1,0:T(8,128)S(1)}, f32[9,512]{1,0:T(8,128)S(1)}, u32[]{:S(2)}, u32[]{:S(2)}) %collective-permute-start.7) | collective-permute-done | bytes 18464 | tf_op jit(solution)/shard_map/ppermute | solution.py:20
  56.7 0.3 copy.63
  57.0 1.0 %gather_fusion.9 = f32[512,9]{1,0:T(8,128)S(1)} fusion(f32[9,1536]{0,1:T(8,128)S(1)} %copy.63, s32[1024]{0:T(1024)S(1)} %pad_clamp_fusion.2), kind=kCustom, calls=%fused_computation.9 | custom fusion | bytes 38912 | tf_op jit(solution)/shard_map/gather | solution.py:39
  58.1 1.0 %gather_fusion.10 = f32[512,9]{1,0:T(8,128)S(1)} fusion(f32[9,1536]{0,1:T(8,128)S(1)} %copy.63, s32[1024]{0:T(1024)S(1)} %pad_clamp_fusion.1), kind=kCustom, calls=%fused_computation.10 | custom fusion | bytes 38912 | tf_op jit(solution)/shard_map/gather | solution.py:39
  59.1 1.0 %gather_fusion.11 = f32[512,9]{1,0:T(8,128)S(1)} fusion(f32[9,1536]{0,1:T(8,128)S(1)} %copy.63, s32[1024]{0:T(1024)S(1)} %pad_clamp_fusion), kind=kCustom, calls=%fused_computation.11 | custom fusion | bytes 38912 | tf_op jit(solution)/shard_map/gather | solution.py:39
  60.1 0.1 multiply_bitcast_fusion.5
  60.5 0.1 multiply_bitcast_fusion.4
  60.6 0.1 copy.66
  60.8 0.1 multiply_bitcast_fusion.3
  61.0 0.1 copy.68
  61.3 1.9 %collective-permute-start.8 = (f32[9,512]{1,0:T(8,128)S(1)}, f32[9,512]{1,0:T(8,128)S(1)}, u32[]{:S(2)}, u32[]{:S(2)}) collective-permute-start(f32[9,512]{1,0:T(8,128)S(1)} %multiply_add_fusion), channel_id=1, source_target_pairs={{0,4},{4,8},{8,12},{12,16},{16,20},{20,24},{24,28},{1,5},{5,9},{9,... | collective-permute-start | bytes 55304 | tf_op jit(solution)/shard_map/ppermute | solution.py:17
  63.2 2.4 %collective-permute-start.9 = (f32[9,512]{1,0:T(8,128)S(1)}, f32[9,512]{1,0:T(8,128)S(1)}, u32[]{:S(2)}, u32[]{:S(2)}) collective-permute-start(f32[9,512]{1,0:T(8,128)S(1)} %multiply_add_fusion), channel_id=1, source_target_pairs={{4,0},{8,4},{12,8},{16,12},{20,16},{24,20},{28,24},{5,1},{9,5},{13... | collective-permute-start | bytes 55304 | tf_op jit(solution)/shard_map/ppermute | solution.py:20
  65.6 2.8 %collective-permute-done.9 = f32[9,512]{1,0:T(8,128)S(1)} collective-permute-done((f32[9,512]{1,0:T(8,128)S(1)}, f32[9,512]{1,0:T(8,128)S(1)}, u32[]{:S(2)}, u32[]{:S(2)}) %collective-permute-start.9) | collective-permute-done | bytes 18464 | tf_op jit(solution)/shard_map/ppermute | solution.py:20
  68.4 0.3 copy.69
  68.7 1.0 %gather_fusion.12 = f32[512,9]{1,0:T(8,128)S(1)} fusion(f32[9,1536]{0,1:T(8,128)S(1)} %copy.69, s32[1024]{0:T(1024)S(1)} %pad_clamp_fusion.2), kind=kCustom, calls=%fused_computation.12 | custom fusion | bytes 38912 | tf_op jit(solution)/shard_map/gather | solution.py:39
  69.8 1.0 %gather_fusion.13 = f32[512,9]{1,0:T(8,128)S(1)} fusion(f32[9,1536]{0,1:T(8,128)S(1)} %copy.69, s32[1024]{0:T(1024)S(1)} %pad_clamp_fusion.1), kind=kCustom, calls=%fused_computation.13 | custom fusion | bytes 38912 | tf_op jit(solution)/shard_map/gather | solution.py:39
  70.8 1.0 %gather_fusion.14 = f32[512,9]{1,0:T(8,128)S(1)} fusion(f32[9,1536]{0,1:T(8,128)S(1)} %copy.69, s32[1024]{0:T(1024)S(1)} %pad_clamp_fusion), kind=kCustom, calls=%fused_computation.14 | custom fusion | bytes 38912 | tf_op jit(solution)/shard_map/gather | solution.py:39
  71.9 0.1 multiply_bitcast_fusion.2
  72.2 0.1 multiply_bitcast_fusion.1
  72.3 0.1 copy.72
  72.5 0.1 multiply_bitcast_fusion
  73.0 0.7 copy-done.4
  73.7 0.8 %convolution_bitcast_fusion = f32[3,15,128]{2,1,0:T(8,128)} fusion(f32[3,3,128]{2,1,0:T(4,128)S(1)} %reshape.394, f32[15,3]{0,1:T(4,128)S(1)} %copy-done.4), kind=kOutput, calls=%fused_computation.15 | convolution fusion | flops 207360 | bytes 27828 | tf_op jit(solution)/shard_map/oc,dcz->doz/dot_general | solution.py:77
  (63 shorter events, 2.8 us)
Async XLA Ops:
  0.0 0.7 copy-start
  0.0 17.4 %copy-start.2 = (bf16[3,9,9,512]{3,0,2,1:T(4,128)(2,1)S(1)}, bf16[3,9,9,512]{3,0,2,1:T(4,128)(2,1)}, u32[]{:S(2)}) copy-start(bf16[3,9,9,512]{3,0,2,1:T(4,128)(2,1)} %param.10) | copy-start | bytes 746500
  9.6 7.7 %copy-start.3 = (s32[3,512]{1,0:T(4,128)S(1)}, s32[3,512]{1,0:T(4,128)}, u32[]{:S(2)}) copy-start(s32[3,512]{1,0:T(4,128)} %param.11) | copy-start | bytes 18436
  9.7 8.2 %collective-permute-start = (f32[9,512]{1,0:T(8,128)S(1)}, f32[9,512]{1,0:T(8,128)S(1)}, u32[]{:S(2)}, u32[]{:S(2)}) collective-permute-start(f32[9,512]{1,0:T(8,128)S(1)} %broadcast_multiply_fusion), channel_id=1, source_target_pairs={{0,4},{4,8},{8,12},{12,16},{16,20},{20,24},{24,28},{1,5},{5,9},{9,... | collective-permute-start | bytes 55304 | tf_op jit(solution)/shard_map/ppermute | solution.py:17
  15.4 5.2 %collective-permute-start.1 = (f32[9,512]{1,0:T(8,128)S(1)}, f32[9,512]{1,0:T(8,128)S(1)}, u32[]{:S(2)}, u32[]{:S(2)}) collective-permute-start(f32[9,512]{1,0:T(8,128)S(1)} %broadcast_multiply_fusion), channel_id=1, source_target_pairs={{4,0},{8,4},{12,8},{16,12},{20,16},{24,20},{28,24},{5,1},{9,5},{13... | collective-permute-start | bytes 55304 | tf_op jit(solution)/shard_map/ppermute | solution.py:20
  25.1 0.9 %copy-start.1 = (bf16[9,9,512]{2,1,0:T(8,128)(2,1)S(1)}, bf16[9,9,512]{2,1,0:T(8,128)(2,1)}, u32[]{:S(2)}) copy-start(bf16[9,9,512]{2,1,0:T(8,128)(2,1)} %param.9) | copy-start | bytes 248836
  26.1 4.3 %collective-permute-start.2 = (f32[9,512]{1,0:T(8,128)S(1)}, f32[9,512]{1,0:T(8,128)S(1)}, u32[]{:S(2)}, u32[]{:S(2)}) collective-permute-start(f32[9,512]{1,0:T(8,128)S(1)} %multiply_add_fusion.3), channel_id=1, source_target_pairs={{0,4},{4,8},{8,12},{12,16},{16,20},{20,24},{24,28},{1,5},{5,9},{9,... | collective-permute-start | bytes 55304 | tf_op jit(solution)/shard_map/ppermute | solution.py:17
  28.0 5.2 %collective-permute-start.3 = (f32[9,512]{1,0:T(8,128)S(1)}, f32[9,512]{1,0:T(8,128)S(1)}, u32[]{:S(2)}, u32[]{:S(2)}) collective-permute-start(f32[9,512]{1,0:T(8,128)S(1)} %multiply_add_fusion.3), channel_id=1, source_target_pairs={{4,0},{8,4},{12,8},{16,12},{20,16},{24,20},{28,24},{5,1},{9,5},{13... | collective-permute-start | bytes 55304 | tf_op jit(solution)/shard_map/ppermute | solution.py:20
  37.8 4.3 %collective-permute-start.4 = (f32[9,512]{1,0:T(8,128)S(1)}, f32[9,512]{1,0:T(8,128)S(1)}, u32[]{:S(2)}, u32[]{:S(2)}) collective-permute-start(f32[9,512]{1,0:T(8,128)S(1)} %multiply_add_fusion.2), channel_id=1, source_target_pairs={{0,4},{4,8},{8,12},{12,16},{16,20},{20,24},{24,28},{1,5},{5,9},{9,... | collective-permute-start | bytes 55304 | tf_op jit(solution)/shard_map/ppermute | solution.py:17
  39.7 5.2 %collective-permute-start.5 = (f32[9,512]{1,0:T(8,128)S(1)}, f32[9,512]{1,0:T(8,128)S(1)}, u32[]{:S(2)}, u32[]{:S(2)}) collective-permute-start(f32[9,512]{1,0:T(8,128)S(1)} %multiply_add_fusion.2), channel_id=1, source_target_pairs={{4,0},{8,4},{12,8},{16,12},{20,16},{24,20},{28,24},{5,1},{9,5},{13... | collective-permute-start | bytes 55304 | tf_op jit(solution)/shard_map/ppermute | solution.py:20
  49.5 4.3 %collective-permute-start.6 = (f32[9,512]{1,0:T(8,128)S(1)}, f32[9,512]{1,0:T(8,128)S(1)}, u32[]{:S(2)}, u32[]{:S(2)}) collective-permute-start(f32[9,512]{1,0:T(8,128)S(1)} %multiply_add_fusion.1), channel_id=1, source_target_pairs={{0,4},{4,8},{8,12},{12,16},{16,20},{20,24},{24,28},{1,5},{5,9},{9,... | collective-permute-start | bytes 55304 | tf_op jit(solution)/shard_map/ppermute | solution.py:17
  51.5 5.2 %collective-permute-start.7 = (f32[9,512]{1,0:T(8,128)S(1)}, f32[9,512]{1,0:T(8,128)S(1)}, u32[]{:S(2)}, u32[]{:S(2)}) collective-permute-start(f32[9,512]{1,0:T(8,128)S(1)} %multiply_add_fusion.1), channel_id=1, source_target_pairs={{4,0},{8,4},{12,8},{16,12},{20,16},{24,20},{28,24},{5,1},{9,5},{13... | collective-permute-start | bytes 55304 | tf_op jit(solution)/shard_map/ppermute | solution.py:20
  61.3 4.3 %collective-permute-start.8 = (f32[9,512]{1,0:T(8,128)S(1)}, f32[9,512]{1,0:T(8,128)S(1)}, u32[]{:S(2)}, u32[]{:S(2)}) collective-permute-start(f32[9,512]{1,0:T(8,128)S(1)} %multiply_add_fusion), channel_id=1, source_target_pairs={{0,4},{4,8},{8,12},{12,16},{16,20},{20,24},{24,28},{1,5},{5,9},{9,... | collective-permute-start | bytes 55304 | tf_op jit(solution)/shard_map/ppermute | solution.py:17
  63.2 5.2 %collective-permute-start.9 = (f32[9,512]{1,0:T(8,128)S(1)}, f32[9,512]{1,0:T(8,128)S(1)}, u32[]{:S(2)}, u32[]{:S(2)}) collective-permute-start(f32[9,512]{1,0:T(8,128)S(1)} %multiply_add_fusion), channel_id=1, source_target_pairs={{4,0},{8,4},{12,8},{16,12},{20,16},{24,20},{28,24},{5,1},{9,5},{13... | collective-permute-start | bytes 55304 | tf_op jit(solution)/shard_map/ppermute | solution.py:20
  73.0 0.7 copy-start.4
where the time goes:
time: 75 us; the launch traced here: 74.5 us
  starting transfers between devices  25 us (33%)
  local copies, waits for them, and re-layouts  21.3 us (28%)
  waiting for transfers between devices  14.1 us (19%)
  blocking collectives  7.06 us (9%)
  other arithmetic  4.68 us (6%)
  matrix products  1.66 us (2%)
  between operations  0.75 us (1%)
    gather x15, local copies, waits for them, and re-layouts, later_sweep(): beside = extended[:, position] * present[None, :]  15.6 us
    ppermute x5, waiting for transfers between devices, extended_2(): lax.ppermute(lax.slice_in_dim(block, 0, width, axis=dim), axis, backward)  14.1 us
    ppermute x5, starting transfers between devices, extended_2(): lax.ppermute(lax.slice_in_dim(block, block.shape[dim] - width, None, axis...  13.4 us
    ppermute x5, starting transfers between devices, extended_2(): lax.ppermute(lax.slice_in_dim(block, 0, width, axis=dim), axis, backward)  11.5 us
    all_gather x1, blocking collectives, local(): coarse_forcing = lax.all_gather(local_rhs, 'grp', axis=1, tiled=True)  7.06 us
    unnamed x10, local copies, waits for them, and re-layouts  2.29 us
    mul x15, other arithmetic, later_sweep(): beside = extended[:, position] * present[None, :]  1.94 us
    mul x15, local copies, waits for them, and re-layouts, later_sweep(): beside = extended[:, position] * present[None, :]  1.66 us
  transfers between devices with their start and end apart: 10, of which 5 were waited for; matrix products, arithmetic and copies ran while one was open for 1% of the time, Pallas kernels for 0%

commit v1 on v0

v1 whole, which is shorter than its diff:
```python
import functools

import jax
import jax.numpy as jnp
from jax import lax
from jax.experimental import pallas as pl
from jax.experimental.pallas import tpu as pltpu
from jax.sharding import PartitionSpec as P

SWEEPS = 6
damping = 0.8
LANES = 128
SUBLANES = 8
COMP = 9
FACES = 3


class Shape:
    def __init__(self, width):
        self.W = width // LANES
        assert self.W * LANES == width and (self.W == 4 or self.W % 8 == 0)
        self.rows = -(-COMP * self.W // SUBLANES) * SUBLANES
        self.NV = self.rows // SUBLANES
        self.Q = max(1, self.W // SUBLANES)
        self.H = max(1, SUBLANES // self.W)
        self.reach = 2 * self.W + 1
        self.TS = 3 * self.W
        self.index_rows = max(SUBLANES, self.W)


def low_half():
    return lax.broadcasted_iota(jnp.int32, (SUBLANES, LANES), 0) < SUBLANES // 2


def restrict_kernel(residual_ref, restriction_ref, out_ref):
    nodes = residual_ref.shape[1]
    diagonal = lax.broadcasted_iota(jnp.int32, (nodes, nodes), 0) == lax.broadcasted_iota(
        jnp.int32, (nodes, nodes), 1
    )
    for m in range(3):
        row = jnp.broadcast_to(restriction_ref[m : m + 1, :], (nodes, nodes))
        column = jnp.sum(jnp.where(diagonal, row, 0.0), axis=1, keepdims=True)
        for v in range(3):
            out_ref[3 * v + m : 3 * v + m + 1, :] = jnp.sum(
                column * residual_ref[v], axis=0, keepdims=True
            )


def prepare_kernel(s, inverse_ref, coupling_ref, neighbours_ref, inv_out, coup_out, lane_out, rel_out):
    width = s.W * LANES
    pad = s.rows - COMP * s.W

    def unpack(matrix, out, where):
        for o in range(s.W):
            piece = matrix[:, o * LANES : (o + 1) * LANES]
            out[where + (pl.ds(o, SUBLANES, stride=s.W), slice(None))] = piece[:SUBLANES]
            out[where + (pl.ds(SUBLANES * s.W + o, 1), slice(None))] = piece[SUBLANES:COMP]
        if pad:
            out[where + (pl.ds(COMP * s.W, pad), slice(None))] = jnp.zeros((pad, LANES), jnp.float32)

    for i in range(COMP):
        unpack(inverse_ref[i].astype(jnp.float32), inv_out, (i,))
        for f in range(FACES):
            unpack(coupling_ref[f, i].astype(jnp.float32), coup_out, (f, i))
    lanes = lax.broadcasted_iota(jnp.int32, (1, LANES), 1)
    for f in range(FACES):
        for o in range(s.W):
            offset = neighbours_ref[f : f + 1, o * LANES : (o + 1) * LANES]
            position = lanes + offset + width
            lane = position & (LANES - 1)
            rel = jnp.where(offset == 0, -1, position >> 7)
            for h in range(s.H):
                row = h * s.W + o
                lane_out[f, row : row + 1, :] = lane
                rel_out[f, row : row + 1, :] = rel


def times(s, matrix, vectors):
    total = [[None] * s.Q for _ in range(COMP)]
    for i in range(COMP):
        for q in range(s.Q):
            acc = None
            for k, packed in enumerate(vectors):
                for v in range(q, s.NV, s.Q):
                    term = matrix(k, i, v) * packed[v]
                    acc = term if acc is None else acc + term
            total[i][q] = acc
    if s.H == 1:
        return [total[v // s.Q][v % s.Q] for v in range(s.NV)]
    low = low_half()
    out = []
    for v in range(s.NV):
        a = total[2 * v][0]
        b = total[2 * v + 1][0] if 2 * v + 1 < COMP else jnp.zeros_like(a)
        out.append(jnp.where(low, a, b) + pltpu.roll(jnp.where(low, b, a), s.W, 0))
    return out


def rows_of(ref, v):
    return ref[v * SUBLANES : (v + 1) * SUBLANES, :]


def first_kernel(s, slots, grp, inverse_ref, *refs):
    pieces, (rhs_out, iterate_out) = refs[:-2], refs[-2:]
    me = lax.axis_index(grp)
    if s.rows > COMP * s.W:
        pad = s.rows - COMP * s.W
        rhs_out[COMP * s.W :, :] = jnp.zeros((pad, LANES), jnp.float32)
    for k, piece in enumerate(pieces):
        slot = slots(me, k)
        rhs_out[pl.ds(slot, SUBLANES, stride=s.W), :] = piece[:SUBLANES, :]
        rhs_out[pl.ds(SUBLANES * s.W + slot, 1), :] = piece[SUBLANES:COMP, :]
    rhs = [rows_of(rhs_out, v) for v in range(s.NV)]
    update = times(s, lambda k, i, v: rows_of(inverse_ref.at[i], v), [rhs])
    for v in range(s.NV):
        iterate_out[v * SUBLANES : (v + 1) * SUBLANES, :] = damping * update[v]


def fill_table(s, table, block, place):
    for j in range(COMP):
        start = j * s.TS + place * s.W
        if s.H == 1:
            for q in range(s.Q):
                table[start + q * SUBLANES : start + (q + 1) * SUBLANES, :] = block[j * s.Q + q]
        else:
            half = (j % s.H) * s.W
            table[start : start + s.W, :] = block[j // s.H][half : half + s.W]


def sweep(s, dom, refs, table):
    inverse_ref, coupling_ref, lane_ref, rel_ref, rhs_ref, iterate_ref, even_ref, odd_ref = refs
    own = [rows_of(iterate_ref, v) for v in range(s.NV)]
    is_even = lax.rem(lax.axis_index(dom), 2) == 0
    pair = [rows_of(even_ref, v) for v in range(s.NV)]
    other = [rows_of(odd_ref, v) for v in range(s.NV)]
    fill_table(s, table, own, 1)
    fill_table(s, table, [jnp.where(is_even, o, p) for p, o in zip(pair, other)], 0)
    fill_table(s, table, [jnp.where(is_even, p, o) for p, o in zip(pair, other)], 2)
    table[COMP * s.TS :, :] = jnp.zeros((SUBLANES, LANES), jnp.float32)
    low = low_half()

    def source(v, r):
        if s.H == 1:
            start = (v // s.Q) * s.TS + (v % s.Q) * SUBLANES + r
            return table[start : start + SUBLANES, :]
        start = 2 * v * s.TS + r
        first = table[start : start + SUBLANES, :]
        if 2 * v + 1 >= COMP:
            return first
        start += s.TS - s.W
        return jnp.where(low, first, table[start : start + SUBLANES, :])

    lane = [[lane_ref[f, q * SUBLANES : (q + 1) * SUBLANES, :] for q in range(s.Q)] for f in range(FACES)]
    rel = [[rel_ref[f, q * SUBLANES : (q + 1) * SUBLANES, :] for q in range(s.Q)] for f in range(FACES)]
    beside = [[jnp.zeros((SUBLANES, LANES), jnp.float32)] * s.NV for _ in range(FACES)]
    for r in range(s.reach):
        here = [[rel[f][q] == r for q in range(s.Q)] for f in range(FACES)]
        for v in range(s.NV):
            tile = source(v, r)
            for f in range(FACES):
                taken = jnp.take_along_axis(tile, lane[f][v % s.Q], axis=1, mode="promise_in_bounds")
                beside[f][v] = jnp.where(here[f][v % s.Q], taken, beside[f][v])
    coupled = times(s, lambda f, i, v: rows_of(coupling_ref.at[f, i], v), beside)
    remain = [rows_of(rhs_ref, v) - coupled[v] for v in range(s.NV)]
    update = times(s, lambda k, i, v: rows_of(inverse_ref.at[i], v), [remain])
    return [(1.0 - damping) * own[v] + damping * update[v] for v in range(s.NV)]


def sweep_kernel(s, dom, *refs):
    out_ref, table = refs[-2:]
    new = sweep(s, dom, refs[:-2], table)
    for v in range(s.NV):
        out_ref[v * SUBLANES : (v + 1) * SUBLANES, :] = new[v]


def last_kernel(s, dom, grp, prolongation_ref, *refs):
    out_ref, table, final = refs[-3:]
    new = sweep(s, dom, refs[:-3], table)
    for v in range(s.NV):
        final[v * SUBLANES : (v + 1) * SUBLANES, :] = new[v]
    me = lax.axis_index(grp)
    rows = [final[pl.ds(j * s.W + me, 1), :] for j in range(COMP)]
    for v in range(3):
        acc = None
        for m in range(3):
            term = prolongation_ref[:, m : m + 1] * rows[3 * v + m]
            acc = term if acc is None else acc + term
        out_ref[v] = acc


def f32(*shape):
    return jax.ShapeDtypeStruct(shape, jnp.float32)


def call(kernel, name, out_shape, scratch=(), flops=0):
    return pl.pallas_call(
        kernel,
        out_shape=out_shape,
        scratch_shapes=scratch,
        compiler_params=pltpu.CompilerParams(vmem_limit_bytes=16 << 20),
        cost_estimate=pl.CostEstimate(flops=flops, bytes_accessed=0, transcendentals=0),
        name=name,
    )


def exchanges(n_dom, n_grp):
    out = []
    for first in (0, 1):
        partner = {d: d for d in range(n_dom)}
        for d in range(first, n_dom - 1, 2):
            partner[d], partner[d + 1] = d + 1, d
        perm = []
        for d in range(n_dom):
            for g in range(n_grp):
                to = g ^ 1 if partner[d] == d and n_grp % 2 == 0 else g
                perm.append((d * n_grp + g, partner[d] * n_grp + to))
        out.append(perm)
    return out


def local(n_dom, n_grp, fine_level_residual, restriction_matrix, prolongation_matrix, block_inverse, face_coupling, neighbours):
    s = Shape(block_inverse.shape[2])
    element_width = fine_level_residual.shape[2]
    assert element_width == LANES and s.W == n_grp
    own = call(restrict_kernel, "restrict", f32(COMP, LANES))(fine_level_residual, restriction_matrix)
    if n_grp & (n_grp - 1) == 0 and n_grp <= 4:
        pieces = [own] + [
            lax.ppermute(own, "grp", [(g, g ^ k) for g in range(n_grp)]) for k in range(1, n_grp)
        ]
        slots = lambda me, k: me ^ k
    else:
        gathered = lax.all_gather(own, "grp", axis=0)
        pieces = [gathered[k] for k in range(n_grp)]
        slots = lambda me, k: k
    inverse, coupling, lane, rel = call(
        functools.partial(prepare_kernel, s),
        "prepare",
        (
            f32(COMP, s.rows, LANES),
            f32(FACES, COMP, s.rows, LANES),
            jax.ShapeDtypeStruct((FACES, s.index_rows, LANES), jnp.int32),
            jax.ShapeDtypeStruct((FACES, s.index_rows, LANES), jnp.int32),
        ),
        flops=20_000_000,
    )(block_inverse, face_coupling, neighbours)
    rhs, iterate = call(
        functools.partial(first_kernel, s, slots, "grp"), "first", (f32(s.rows, LANES), f32(s.rows, LANES))
    )(inverse, *pieces)
    even, odd = exchanges(n_dom, n_grp)
    table = pltpu.VMEM((COMP * s.TS + SUBLANES, LANES), jnp.float32)
    for index in range(1, SWEEPS):
        pair = lax.ppermute(iterate, ("dom", "grp"), even)
        other = lax.ppermute(iterate, ("dom", "grp"), odd)
        operands = (inverse, coupling, lane, rel, rhs, iterate, pair, other)
        if index < SWEEPS - 1:
            iterate = call(
                functools.partial(sweep_kernel, s, "dom"), "sweep", f32(s.rows, LANES), (table,)
            )(*operands)
    return call(
        functools.partial(last_kernel, s, "dom", "grp"),
        "last",
        f32(3, prolongation_matrix.shape[0], LANES),
        (table, pltpu.VMEM((s.rows, LANES), jnp.float32)),
    )(prolongation_matrix, *operands)


def solution(mesh):
    placed = (
        P(None, None, ("dom", "grp")),
        P(),
        P(),
        P(None, None, "dom"),
        P(None, None, None, "dom"),
        P(None, "dom"),
    )
    return jax.shard_map(
        functools.partial(local, mesh.shape["dom"], mesh.shape["grp"]),
        mesh=mesh,
        in_specs=placed,
        out_specs=P(None, None, ("dom", "grp")),
        check_vma=False,
    )
```

time: 75 us -> 33.3 us (0.44)
  local copies, waits for them, and re-layouts: 21.3 us -> 2.58 us
  starting transfers between devices: 25 us -> 11.5 us
  blocking collectives: 7.06 us -> 0 us
  other arithmetic: 4.68 us -> 0 us
  Pallas kernels: 0 us -> 2.92 us
  matrix products: 1.66 us -> 0 us
  waiting for transfers between devices: 14.1 us -> 15.5 us
    gather x15 -> x0, local copies, waits for them, and re-layouts: 15.6 us -> none  [later_sweep(): beside = extended[:, position] * present[None, :]]
    ppermute x10 -> x13, starting transfers between devices: 25 us -> 11.5 us  [the longest x5 5.16 us: local(): pair = lax.ppermute(iterate, ('dom', 'grp'), even)]
    all_gather x1 -> x0, blocking collectives: 7.06 us -> none  [local(): coarse_forcing = lax.all_gather(local_rhs, 'grp', axis=1, tiled=True)]
    pallas_call x0 -> x8, Pallas kernels: none -> 2.92 us  [the longest x4 1.63 us: local(): call(functools.partial(sweep_kernel, s, 'dom'), 'sweep', f32(s.rows, LANE...]
    reduce_sum x20 -> x0, other arithmetic: 2.52 us -> none  [the longest x6 1.33 us: apply_inverse(): jnp.sum(block_inverse.astype(jnp.float32) * remain[None, :, :], axis=1)]
    mul x16 -> x0, other arithmetic: 1.95 us -> none  [the longest x15 1.94 us: later_sweep(): beside = extended[:, position] * present[None, :]]
    mul x15 -> x0, local copies, waits for them, and re-layouts: 1.66 us -> none  [later_sweep(): beside = extended[:, position] * present[None, :]]
    dot_general x2 -> x0, matrix products: 1.66 us -> none  [the longest x1 0.84 us: local(): jnp.einsum('oc,dcz->doz', prolongation_matrix, owned_elements.reshape(3,...]
  transfers between devices with their start and end apart: 10 -> 13, of which waited for: 5 -> 8; matrix products, arithmetic and copies ran while one was open for 1% -> 4% of each run, Pallas kernels for 0% -> 0%
where the time goes in v1:
time: 33.3 us; the launch traced here: 32.7 us
  waiting for transfers between devices  15.5 us (47%)
  starting transfers between devices  11.5 us (35%)
  Pallas kernels  2.92 us (9%)
  local copies, waits for them, and re-layouts  2.58 us (8%)
    ppermute x5, waiting for transfers between devices, local(): other = lax.ppermute(iterate, ('dom', 'grp'), odd)  12.2 us
    ppermute x5, starting transfers between devices, local(): pair = lax.ppermute(iterate, ('dom', 'grp'), even)  5.16 us
    ppermute x3, starting transfers between devices, local(): lax.ppermute(own, 'grp', [(g, g ^ k) for g in range(n_grp)])  3.35 us
    ppermute x5, starting transfers between devices, local(): other = lax.ppermute(iterate, ('dom', 'grp'), odd)  3 us
    unnamed x12, local copies, waits for them, and re-layouts  2.58 us
    ppermute x3, waiting for transfers between devices, local(): lax.ppermute(own, 'grp', [(g, g ^ k) for g in range(n_grp)])  2.18 us
    pallas_call x4, Pallas kernels, local(): call(functools.partial(sweep_kernel, s, 'dom'), 'sweep', f32(s.rows, LANE...  1.63 us
    ppermute x5, waiting for transfers between devices, local(): pair = lax.ppermute(iterate, ('dom', 'grp'), even)  1.13 us
  transfers between devices with their start and end apart: 13, of which 8 were waited for; matrix products, arithmetic and copies ran while one was open for 4% of the time, Pallas kernels for 0%

profile of v1, /device:TPU:1, one launch (start us, length us, event | category | flops | bytes accessed | tf_op | source)
XLA Modules:
  0.0 32.7 jit_solution(18427344966654049779)
XLA Ops:
  0.0 0.0 copy-start.1
  0.0 0.7 %copy-done.1 = f32[3,15,128]{2,1,0:T(8,128)S(1)} copy-done((f32[3,15,128]{2,1,0:T(8,128)S(1)}, f32[3,15,128]{2,1,0:T(8,128)}, u32[]{:S(2)}) %copy-start.1) | copy-done | bytes 23064
  0.7 0.0 copy-start.3
  0.7 0.7 %copy-done.3 = f32[3,15]{1,0:T(4,128)S(1)} copy-done((f32[3,15]{1,0:T(4,128)S(1)}, f32[3,15]{1,0:T(4,128)}, u32[]{:S(2)}) %copy-start.3) | copy-done | bytes 204
  1.4 0.1 restrict.1.refs_0_
  1.5 0.0 copy-start
  1.5 0.0 copy-start.2
  1.5 2.1 %collective-permute-start = (f32[9,128]{1,0:T(8,128)S(1)}, f32[9,128]{1,0:T(8,128)S(1)}, u32[]{:S(2)}, u32[]{:S(2)}) collective-permute-start(f32[9,128]{1,0:T(8,128)S(1)} %restrict.1.refs_0_), channel_id=1, source_target_pairs={{0,1},{1,0},{2,3},{3,2},{4,5},{5,4},{6,7},{7,6},{8,9},{9,8},{10,11... | collective-permute-start | bytes 13832 | tf_op jit(solution)/shard_map/ppermute | solution.py:228
  3.6 1.2 %collective-permute-start.1 = (f32[9,128]{1,0:T(8,128)S(1)}, f32[9,128]{1,0:T(8,128)S(1)}, u32[]{:S(2)}, u32[]{:S(2)}) collective-permute-start(f32[9,128]{1,0:T(8,128)S(1)} %restrict.1.refs_0_), channel_id=1, source_target_pairs={{0,2},{1,3},{2,0},{3,1},{4,6},{5,7},{6,4},{7,5},{8,10},{9,11},{10,... | collective-permute-start | bytes 13832 | tf_op jit(solution)/shard_map/ppermute | solution.py:228
  4.9 0.0 collective-permute-start.2
  4.9 1.1 %copy.7.coupling_ref = bf16[3,9,9,512]{3,2,1,0:T(8,128)(2,1)S(1)} copy(bf16[3,9,9,512]{3,0,2,1:T(4,128)(2,1)} %param.10) | data formatting | bytes 497664 | tf_op args[4]
  6.0 0.0 copy-done
  6.0 0.0 copy-done.2
  6.0 0.1 prepare.1
  6.1 0.0 collective-permute-done.refs_1_
  6.1 0.0 collective-permute-done.1.refs_2_
  6.1 2.1 %collective-permute-done.2.refs_3_ = f32[9,128]{1,0:T(8,128)S(1)} collective-permute-done((f32[9,128]{1,0:T(8,128)S(1)}, f32[9,128]{1,0:T(8,128)S(1)}, u32[]{:S(2)}, u32[]{:S(2)}) %collective-permute-start.2) | collective-permute-done | bytes 4640 | tf_op jit(solution)/shard_map/ppermute | solution.py:228
  8.3 2.5 %collective-permute-start.3 = (f32[40,128]{1,0:T(8,128)S(1)}, f32[40,128]{1,0:T(8,128)S(1)}, u32[]{:S(2)}, u32[]{:S(2)}) collective-permute-start(f32[40,128]{1,0:T(8,128)S(1)} %get-tuple-element.16.refs_5_), channel_id=1, source_target_pairs={{0,4},{1,5},{2,6},{3,7},{4,0},{5,1},{6,2},{7,3},{8,12},{9,13},{10,... | collective-permute-start | bytes 61448 | tf_op jit(solution)/shard_map/ppermute | solution.py:252
  10.8 1.3 %collective-permute-start.4 = (f32[40,128]{1,0:T(8,128)S(1)}, f32[40,128]{1,0:T(8,128)S(1)}, u32[]{:S(2)}, u32[]{:S(2)}) collective-permute-start(f32[40,128]{1,0:T(8,128)S(1)} %get-tuple-element.16.refs_5_), channel_id=1, source_target_pairs={{0,1},{1,0},{2,3},{3,2},{4,8},{5,9},{6,10},{7,11},{8,4},{9,5},{10,... | collective-permute-start | bytes 61448 | tf_op jit(solution)/shard_map/ppermute | solution.py:253
  12.0 0.0 collective-permute-done.3.refs_6_
  12.0 2.2 %collective-permute-done.4.refs_7_ = f32[40,128]{1,0:T(8,128)S(1)} collective-permute-done((f32[40,128]{1,0:T(8,128)S(1)}, f32[40,128]{1,0:T(8,128)S(1)}, u32[]{:S(2)}, u32[]{:S(2)}) %collective-permute-start.4) | collective-permute-done | bytes 20512 | tf_op jit(solution)/shard_map/ppermute | solution.py:253
  14.2 0.4 %sweep.4.refs_5_ = f32[40,128]{1,0:T(8,128)S(1)} custom-call(f32[9,40,128]{2,1,0:T(8,128)S(1)} %get-tuple-element.11.inverse_ref.refs_0_, f32[3,9,40,128]{3,2,1,0:T(8,128)S(1)} %get-tuple-element.12.refs_1_, s32[3,8,128]{2,1,0:T(8,128)S(1)} %get-tuple-element.13.refs_2_, s32[3,8,128]{2,1,0:T(8,128)S(1)} %get-tuple-element.14.refs_3_, ...), custom_call_target="tpu_custom_call" | custom-call | tf_op jit(solution)/shard_map/sweep/pallas_call | solution.py:256
  14.6 0.5 %collective-permute-start.5 = (f32[40,128]{1,0:T(8,128)S(1)}, f32[40,128]{1,0:T(8,128)S(1)}, u32[]{:S(2)}, u32[]{:S(2)}) collective-permute-start(f32[40,128]{1,0:T(8,128)S(1)} %sweep.4.refs_5_), channel_id=1, source_target_pairs={{0,4},{1,5},{2,6},{3,7},{4,0},{5,1},{6,2},{7,3},{8,12},{9,13},{10,... | collective-permute-start | bytes 61448 | tf_op jit(solution)/shard_map/ppermute | solution.py:252
  15.1 1.0 %collective-permute-start.6 = (f32[40,128]{1,0:T(8,128)S(1)}, f32[40,128]{1,0:T(8,128)S(1)}, u32[]{:S(2)}, u32[]{:S(2)}) collective-permute-start(f32[40,128]{1,0:T(8,128)S(1)} %sweep.4.refs_5_), channel_id=1, source_target_pairs={{0,1},{1,0},{2,3},{3,2},{4,8},{5,9},{6,10},{7,11},{8,4},{9,5},{10,... | collective-permute-start | bytes 61448 | tf_op jit(solution)/shard_map/ppermute | solution.py:253
  16.1 0.0 collective-permute-done.5.refs_6_
  16.1 2.5 %collective-permute-done.6.refs_7_ = f32[40,128]{1,0:T(8,128)S(1)} collective-permute-done((f32[40,128]{1,0:T(8,128)S(1)}, f32[40,128]{1,0:T(8,128)S(1)}, u32[]{:S(2)}, u32[]{:S(2)}) %collective-permute-start.6) | collective-permute-done | bytes 20512 | tf_op jit(solution)/shard_map/ppermute | solution.py:253
  18.6 0.4 %sweep.5.refs_5_ = f32[40,128]{1,0:T(8,128)S(1)} custom-call(f32[9,40,128]{2,1,0:T(8,128)S(1)} %get-tuple-element.11.inverse_ref.refs_0_, f32[3,9,40,128]{3,2,1,0:T(8,128)S(1)} %get-tuple-element.12.refs_1_, s32[3,8,128]{2,1,0:T(8,128)S(1)} %get-tuple-element.13.refs_2_, s32[3,8,128]{2,1,0:T(8,128)S(1)} %get-tuple-element.14.refs_3_, ...), custom_call_target="tpu_custom_call" | custom-call | tf_op jit(solution)/shard_map/sweep/pallas_call | solution.py:256
  19.0 0.5 %collective-permute-start.7 = (f32[40,128]{1,0:T(8,128)S(1)}, f32[40,128]{1,0:T(8,128)S(1)}, u32[]{:S(2)}, u32[]{:S(2)}) collective-permute-start(f32[40,128]{1,0:T(8,128)S(1)} %sweep.5.refs_5_), channel_id=1, source_target_pairs={{0,4},{1,5},{2,6},{3,7},{4,0},{5,1},{6,2},{7,3},{8,12},{9,13},{10,... | collective-permute-start | bytes 61448 | tf_op jit(solution)/shard_map/ppermute | solution.py:252
  19.5 0.5 %collective-permute-start.8 = (f32[40,128]{1,0:T(8,128)S(1)}, f32[40,128]{1,0:T(8,128)S(1)}, u32[]{:S(2)}, u32[]{:S(2)}) collective-permute-start(f32[40,128]{1,0:T(8,128)S(1)} %sweep.5.refs_5_), channel_id=1, source_target_pairs={{0,1},{1,0},{2,3},{3,2},{4,8},{5,9},{6,10},{7,11},{8,4},{9,5},{10,... | collective-permute-start | bytes 61448 | tf_op jit(solution)/shard_map/ppermute | solution.py:253
  19.9 0.4 %collective-permute-done.7.refs_6_ = f32[40,128]{1,0:T(8,128)S(1)} collective-permute-done((f32[40,128]{1,0:T(8,128)S(1)}, f32[40,128]{1,0:T(8,128)S(1)}, u32[]{:S(2)}, u32[]{:S(2)}) %collective-permute-start.7) | collective-permute-done | bytes 20512 | tf_op jit(solution)/shard_map/ppermute | solution.py:252
  20.3 2.7 %collective-permute-done.8.refs_7_ = f32[40,128]{1,0:T(8,128)S(1)} collective-permute-done((f32[40,128]{1,0:T(8,128)S(1)}, f32[40,128]{1,0:T(8,128)S(1)}, u32[]{:S(2)}, u32[]{:S(2)}) %collective-permute-start.8) | collective-permute-done | bytes 20512 | tf_op jit(solution)/shard_map/ppermute | solution.py:253
  23.0 0.4 %sweep.6.refs_5_ = f32[40,128]{1,0:T(8,128)S(1)} custom-call(f32[9,40,128]{2,1,0:T(8,128)S(1)} %get-tuple-element.11.inverse_ref.refs_0_, f32[3,9,40,128]{3,2,1,0:T(8,128)S(1)} %get-tuple-element.12.refs_1_, s32[3,8,128]{2,1,0:T(8,128)S(1)} %get-tuple-element.13.refs_2_, s32[3,8,128]{2,1,0:T(8,128)S(1)} %get-tuple-element.14.refs_3_, ...), custom_call_target="tpu_custom_call" | custom-call | tf_op jit(solution)/shard_map/sweep/pallas_call | solution.py:256
  23.4 0.0 copy-start.4
  23.4 0.2 collective-permute-start.10
  23.6 0.8 %collective-permute-start.9 = (f32[40,128]{1,0:T(8,128)S(1)}, f32[40,128]{1,0:T(8,128)S(1)}, u32[]{:S(2)}, u32[]{:S(2)}) collective-permute-start(f32[40,128]{1,0:T(8,128)S(1)} %sweep.6.refs_5_), channel_id=1, source_target_pairs={{0,4},{1,5},{2,6},{3,7},{4,0},{5,1},{6,2},{7,3},{8,12},{9,13},{10,... | collective-permute-start | bytes 61448 | tf_op jit(solution)/shard_map/ppermute | solution.py:252
  24.4 2.3 %collective-permute-done.10.refs_7_ = f32[40,128]{1,0:T(8,128)S(1)} collective-permute-done((f32[40,128]{1,0:T(8,128)S(1)}, f32[40,128]{1,0:T(8,128)S(1)}, u32[]{:S(2)}, u32[]{:S(2)}) %collective-permute-start.10) | collective-permute-done | bytes 20512 | tf_op jit(solution)/shard_map/ppermute | solution.py:253
  26.7 0.0 collective-permute-done.9.refs_6_
  26.7 0.4 %sweep.7.refs_5_ = f32[40,128]{1,0:T(8,128)S(1)} custom-call(f32[9,40,128]{2,1,0:T(8,128)S(1)} %get-tuple-element.11.inverse_ref.refs_0_, f32[3,9,40,128]{3,2,1,0:T(8,128)S(1)} %get-tuple-element.12.refs_1_, s32[3,8,128]{2,1,0:T(8,128)S(1)} %get-tuple-element.13.refs_2_, s32[3,8,128]{2,1,0:T(8,128)S(1)} %get-tuple-element.14.refs_3_, ...), custom_call_target="tpu_custom_call" | custom-call | tf_op jit(solution)/shard_map/sweep/pallas_call | solution.py:256
  27.1 1.0 %collective-permute-start.11 = (f32[40,128]{1,0:T(8,128)S(1)}, f32[40,128]{1,0:T(8,128)S(1)}, u32[]{:S(2)}, u32[]{:S(2)}) collective-permute-start(f32[40,128]{1,0:T(8,128)S(1)} %sweep.7.refs_5_), channel_id=1, source_target_pairs={{0,4},{1,5},{2,6},{3,7},{4,0},{5,1},{6,2},{7,3},{8,12},{9,13},{10,... | collective-permute-start | bytes 61448 | tf_op jit(solution)/shard_map/ppermute | solution.py:252
  28.1 0.0 collective-permute-start.12
  28.1 0.0 copy-done.4
  28.1 0.1 copy.8.prolongation_ref
  28.2 0.7 %collective-permute-done.11.refs_6_ = f32[40,128]{1,0:T(8,128)S(1)} collective-permute-done((f32[40,128]{1,0:T(8,128)S(1)}, f32[40,128]{1,0:T(8,128)S(1)}, u32[]{:S(2)}, u32[]{:S(2)}) %collective-permute-start.11) | collective-permute-done | bytes 20512 | tf_op jit(solution)/shard_map/ppermute | solution.py:252
  29.0 2.6 %collective-permute-done.12.refs_7_ = f32[40,128]{1,0:T(8,128)S(1)} collective-permute-done((f32[40,128]{1,0:T(8,128)S(1)}, f32[40,128]{1,0:T(8,128)S(1)}, u32[]{:S(2)}, u32[]{:S(2)}) %collective-permute-start.12) | collective-permute-done | bytes 20512 | tf_op jit(solution)/shard_map/ppermute | solution.py:253
  31.6 1.1 %last.1 = f32[3,15,128]{2,1,0:T(8,128)} custom-call(f32[15,3]{1,0:T(8,128)S(1)} %copy.8.prolongation_ref, f32[9,40,128]{2,1,0:T(8,128)S(1)} %get-tuple-element.11.inverse_ref.refs_0_, f32[3,9,40,128]{3,2,1,0:T(8,128)S(1)} %get-tuple-element.12.refs_1_, s32[3,8,128]{2,1,0:T(8,128)S(1)} %get-tuple-element.13.refs_2_, ...), custom_call_target="tpu_custom_call" | custom-call | tf_op jit(solution)/shard_map/last/pallas_call | solution.py:259
  (1 shorter events, 0.0 us)
Async XLA Ops:
  0.0 0.7 %copy-start.1 = (f32[3,15,128]{2,1,0:T(8,128)S(1)}, f32[3,15,128]{2,1,0:T(8,128)}, u32[]{:S(2)}) copy-start(f32[3,15,128]{2,1,0:T(8,128)} %residual_ref.1) | copy-start | bytes 69124
  0.7 0.7 %copy-start.3 = (f32[3,15]{1,0:T(4,128)S(1)}, f32[3,15]{1,0:T(4,128)}, u32[]{:S(2)}) copy-start(f32[3,15]{1,0:T(4,128)} %restriction_ref.1) | copy-start | bytes 544
  1.5 4.4 %copy-start = (bf16[9,9,512]{2,1,0:T(8,128)(2,1)S(1)}, bf16[9,9,512]{2,1,0:T(8,128)(2,1)}, u32[]{:S(2)}) copy-start(bf16[9,9,512]{2,1,0:T(8,128)(2,1)} %inverse_ref.1) | copy-start | bytes 248836
  1.5 4.4 %copy-start.2 = (s32[3,512]{1,0:T(4,128)S(1)}, s32[3,512]{1,0:T(4,128)}, u32[]{:S(2)}) copy-start(s32[3,512]{1,0:T(4,128)} %neighbours_ref.1) | copy-start | bytes 18436
  1.5 4.5 %collective-permute-start = (f32[9,128]{1,0:T(8,128)S(1)}, f32[9,128]{1,0:T(8,128)S(1)}, u32[]{:S(2)}, u32[]{:S(2)}) collective-permute-start(f32[9,128]{1,0:T(8,128)S(1)} %restrict.1.refs_0_), channel_id=1, source_target_pairs={{0,1},{1,0},{2,3},{3,2},{4,5},{5,4},{6,7},{7,6},{8,9},{9,8},{10,11... | collective-permute-start | bytes 13832 | tf_op jit(solution)/shard_map/ppermute | solution.py:228
  3.6 2.5 %collective-permute-start.1 = (f32[9,128]{1,0:T(8,128)S(1)}, f32[9,128]{1,0:T(8,128)S(1)}, u32[]{:S(2)}, u32[]{:S(2)}) collective-permute-start(f32[9,128]{1,0:T(8,128)S(1)} %restrict.1.refs_0_), channel_id=1, source_target_pairs={{0,2},{1,3},{2,0},{3,1},{4,6},{5,7},{6,4},{7,5},{8,10},{9,11},{10,... | collective-permute-start | bytes 13832 | tf_op jit(solution)/shard_map/ppermute | solution.py:228
  4.9 3.4 %collective-permute-start.2 = (f32[9,128]{1,0:T(8,128)S(1)}, f32[9,128]{1,0:T(8,128)S(1)}, u32[]{:S(2)}, u32[]{:S(2)}) collective-permute-start(f32[9,128]{1,0:T(8,128)S(1)} %restrict.1.refs_0_), channel_id=1, source_target_pairs={{0,3},{1,2},{2,1},{3,0},{4,7},{5,6},{6,5},{7,4},{8,11},{9,10},{10,... | collective-permute-start | bytes 13832 | tf_op jit(solution)/shard_map/ppermute | solution.py:228
  8.3 3.7 %collective-permute-start.3 = (f32[40,128]{1,0:T(8,128)S(1)}, f32[40,128]{1,0:T(8,128)S(1)}, u32[]{:S(2)}, u32[]{:S(2)}) collective-permute-start(f32[40,128]{1,0:T(8,128)S(1)} %get-tuple-element.16.refs_5_), channel_id=1, source_target_pairs={{0,4},{1,5},{2,6},{3,7},{4,0},{5,1},{6,2},{7,3},{8,12},{9,13},{10,... | collective-permute-start | bytes 61448 | tf_op jit(solution)/shard_map/ppermute | solution.py:252
  10.8 3.5 %collective-permute-start.4 = (f32[40,128]{1,0:T(8,128)S(1)}, f32[40,128]{1,0:T(8,128)S(1)}, u32[]{:S(2)}, u32[]{:S(2)}) collective-permute-start(f32[40,128]{1,0:T(8,128)S(1)} %get-tuple-element.16.refs_5_), channel_id=1, source_target_pairs={{0,1},{1,0},{2,3},{3,2},{4,8},{5,9},{6,10},{7,11},{8,4},{9,5},{10,... | collective-permute-start | bytes 61448 | tf_op jit(solution)/shard_map/ppermute | solution.py:253
  14.6 1.5 %collective-permute-start.5 = (f32[40,128]{1,0:T(8,128)S(1)}, f32[40,128]{1,0:T(8,128)S(1)}, u32[]{:S(2)}, u32[]{:S(2)}) collective-permute-start(f32[40,128]{1,0:T(8,128)S(1)} %sweep.4.refs_5_), channel_id=1, source_target_pairs={{0,4},{1,5},{2,6},{3,7},{4,0},{5,1},{6,2},{7,3},{8,12},{9,13},{10,... | collective-permute-start | bytes 61448 | tf_op jit(solution)/shard_map/ppermute | solution.py:252
  15.1 3.5 %collective-permute-start.6 = (f32[40,128]{1,0:T(8,128)S(1)}, f32[40,128]{1,0:T(8,128)S(1)}, u32[]{:S(2)}, u32[]{:S(2)}) collective-permute-start(f32[40,128]{1,0:T(8,128)S(1)} %sweep.4.refs_5_), channel_id=1, source_target_pairs={{0,1},{1,0},{2,3},{3,2},{4,8},{5,9},{6,10},{7,11},{8,4},{9,5},{10,... | collective-permute-start | bytes 61448 | tf_op jit(solution)/shard_map/ppermute | solution.py:253
  19.0 1.3 %collective-permute-start.7 = (f32[40,128]{1,0:T(8,128)S(1)}, f32[40,128]{1,0:T(8,128)S(1)}, u32[]{:S(2)}, u32[]{:S(2)}) collective-permute-start(f32[40,128]{1,0:T(8,128)S(1)} %sweep.5.refs_5_), channel_id=1, source_target_pairs={{0,4},{1,5},{2,6},{3,7},{4,0},{5,1},{6,2},{7,3},{8,12},{9,13},{10,... | collective-permute-start | bytes 61448 | tf_op jit(solution)/shard_map/ppermute | solution.py:252
  19.5 3.5 %collective-permute-start.8 = (f32[40,128]{1,0:T(8,128)S(1)}, f32[40,128]{1,0:T(8,128)S(1)}, u32[]{:S(2)}, u32[]{:S(2)}) collective-permute-start(f32[40,128]{1,0:T(8,128)S(1)} %sweep.5.refs_5_), channel_id=1, source_target_pairs={{0,1},{1,0},{2,3},{3,2},{4,8},{5,9},{6,10},{7,11},{8,4},{9,5},{10,... | collective-permute-start | bytes 61448 | tf_op jit(solution)/shard_map/ppermute | solution.py:253
  23.4 4.7 %copy-start.4 = (f32[15,3]{0,1:T(4,128)S(1)}, f32[15,3]{0,1:T(4,128)}, u32[]{:S(2)}) copy-start(f32[15,3]{0,1:T(4,128)} %param.8) | copy-start | bytes 544
  23.4 3.3 %collective-permute-start.10 = (f32[40,128]{1,0:T(8,128)S(1)}, f32[40,128]{1,0:T(8,128)S(1)}, u32[]{:S(2)}, u32[]{:S(2)}) collective-permute-start(f32[40,128]{1,0:T(8,128)S(1)} %sweep.6.refs_5_), channel_id=1, source_target_pairs={{0,1},{1,0},{2,3},{3,2},{4,8},{5,9},{6,10},{7,11},{8,4},{9,5},{10,... | collective-permute-start | bytes 61448 | tf_op jit(solution)/shard_map/ppermute | solution.py:253
  23.6 3.0 %collective-permute-start.9 = (f32[40,128]{1,0:T(8,128)S(1)}, f32[40,128]{1,0:T(8,128)S(1)}, u32[]{:S(2)}, u32[]{:S(2)}) collective-permute-start(f32[40,128]{1,0:T(8,128)S(1)} %sweep.6.refs_5_), channel_id=1, source_target_pairs={{0,4},{1,5},{2,6},{3,7},{4,0},{5,1},{6,2},{7,3},{8,12},{9,13},{10,... | collective-permute-start | bytes 61448 | tf_op jit(solution)/shard_map/ppermute | solution.py:252
  27.1 1.9 %collective-permute-start.11 = (f32[40,128]{1,0:T(8,128)S(1)}, f32[40,128]{1,0:T(8,128)S(1)}, u32[]{:S(2)}, u32[]{:S(2)}) collective-permute-start(f32[40,128]{1,0:T(8,128)S(1)} %sweep.7.refs_5_), channel_id=1, source_target_pairs={{0,4},{1,5},{2,6},{3,7},{4,0},{5,1},{6,2},{7,3},{8,12},{9,13},{10,... | collective-permute-start | bytes 61448 | tf_op jit(solution)/shard_map/ppermute | solution.py:252
  28.1 3.5 %collective-permute-start.12 = (f32[40,128]{1,0:T(8,128)S(1)}, f32[40,128]{1,0:T(8,128)S(1)}, u32[]{:S(2)}, u32[]{:S(2)}) collective-permute-start(f32[40,128]{1,0:T(8,128)S(1)} %sweep.7.refs_5_), channel_id=1, source_target_pairs={{0,1},{1,0},{2,3},{3,2},{4,8},{5,9},{6,10},{7,11},{8,4},{9,5},{10,... | collective-permute-start | bytes 61448 | tf_op jit(solution)/shard_map/ppermute | solution.py:253

commit v2 on v1

v2 whole, which is shorter than its diff:
```python
import functools

import jax
import jax.numpy as jnp
from jax import lax
from jax.experimental import pallas as pl
from jax.experimental.pallas import tpu as pltpu
from jax.sharding import PartitionSpec as P


SWEEPS = 6
damping = 0.8
LANES = 128
SUBLANES = 8
COMP = 9
FACES = 3


class Shape:
    def __init__(self, width):
        self.W = width // LANES
        assert self.W * LANES == width and (self.W == 4 or self.W % 8 == 0)
        self.rows = -(-COMP * self.W // SUBLANES) * SUBLANES
        self.NV = self.rows // SUBLANES
        self.Q = max(1, self.W // SUBLANES)
        self.H = max(1, SUBLANES // self.W)
        self.index_rows = max(SUBLANES, self.W)
        self.table_rows = 2 * COMP * self.W + 2 * SUBLANES if self.H == 1 else 2 * (self.rows + SUBLANES)


def place_of_row(s):
    row = lax.broadcasted_iota(jnp.int32, (SUBLANES, LANES), 0)
    return row & (s.W - 1) if s.H > 1 else row


def load(sources, targets, sems):
    copies = [
        pltpu.make_async_copy(source, target, sems.at[n]) for n, (source, target) in enumerate(zip(sources, targets))
    ]
    for copy in copies:
        copy.start()
    for copy in copies:
        copy.wait()


def restrict_kernel(residual_hbm, restriction_hbm, out_ref, residual_ref, restriction_ref, sems):
    load((residual_hbm, restriction_hbm), (residual_ref, restriction_ref), sems)
    nodes = residual_ref.shape[1]
    diagonal = lax.broadcasted_iota(jnp.int32, (nodes, nodes), 0) == lax.broadcasted_iota(
        jnp.int32, (nodes, nodes), 1
    )
    for m in range(3):
        row = jnp.broadcast_to(restriction_ref[m : m + 1, :], (nodes, nodes))
        column = jnp.sum(jnp.where(diagonal, row, 0.0), axis=1, keepdims=True)
        for v in range(3):
            out_ref[3 * v + m : 3 * v + m + 1, :] = jnp.sum(
                column * residual_ref[v], axis=0, keepdims=True
            )


def prepare_kernel(s, dom, *refs):
    sources, targets, sems = refs[:3], refs[-4:-1], refs[-1]
    inv_out, spread_out, coup_out, lane_out, own_out, halo_out, even_out = refs[3:-4]
    inverse_ref, coupling_ref, neighbours_ref = targets
    load(sources, targets, sems)
    width = s.W * LANES
    pad = s.rows - COMP * s.W
    zeros = jnp.zeros((max(pad, 1), LANES), jnp.float32)
    for i in range(COMP):
        matrix = inverse_ref[i].astype(jnp.float32)
        for o in range(s.W):
            piece = matrix[:, o * LANES : (o + 1) * LANES]
            inv_out[i, pl.ds(o, SUBLANES, stride=s.W), :] = piece[:SUBLANES]
            inv_out[i, SUBLANES * s.W + o : SUBLANES * s.W + o + 1, :] = piece[SUBLANES:COMP]
            for h in range(s.H):
                row = h * s.W + o
                spread_out[i, pl.ds(row, SUBLANES, stride=s.index_rows), :] = piece[:SUBLANES]
                row += SUBLANES * s.index_rows
                spread_out[i, row : row + 1, :] = piece[SUBLANES:COMP]
        if pad:
            inv_out[i, COMP * s.W :, :] = zeros
            for f in range(FACES):
                start = (f * COMP + i) * s.rows + COMP * s.W
                coup_out[start : start + pad, :] = zeros
        for j in range(COMP):
            matrix = coupling_ref[i, j].astype(jnp.float32)
            for o in range(s.W):
                coup_out[pl.ds(i * s.rows + j * s.W + o, FACES, stride=COMP * s.rows), :] = matrix[
                    :, o * LANES : (o + 1) * LANES
                ]
    lanes = lax.broadcasted_iota(jnp.int32, (1, LANES), 1)
    for f in range(FACES):
        for o in range(s.W):
            offset = neighbours_ref[f : f + 1, o * LANES : (o + 1) * LANES]
            position = lanes + offset + width
            reach = position >> 7
            tile = reach + o
            inside = (tile >= s.W) & (tile < 2 * s.W)
            wall = offset == 0
            lane = position & (LANES - 1)
            own = jnp.where(wall | ~inside, -1, reach & (s.W - 1))
            halo = jnp.where(wall | inside, -1, jnp.where(tile < s.W, reach, reach - s.W))
            for h in range(s.H):
                row = h * s.W + o
                lane_out[f, row : row + 1, :] = lane
                own_out[f, row : row + 1, :] = own
                halo_out[f, row : row + 1, :] = halo
    even_out[...] = jnp.full((SUBLANES, LANES), 1 - (lax.axis_index(dom) & 1), jnp.int32)


def rows_of(ref, v):
    return ref[v * SUBLANES : (v + 1) * SUBLANES, :]


def times(s, matrix, vectors):
    total = [[None] * s.Q for _ in range(COMP)]
    for i in range(COMP):
        for q in range(s.Q):
            acc = None
            for k, packed in enumerate(vectors):
                for v in range(q, s.NV, s.Q):
                    term = matrix(k, i, v) * packed[v]
                    acc = term if acc is None else acc + term
            total[i][q] = acc
    if s.H == 1:
        return [total[v // s.Q][v % s.Q] for v in range(s.NV)]
    low = lax.broadcasted_iota(jnp.int32, (SUBLANES, LANES), 0) < s.W
    out = []
    for v in range(s.NV):
        a = total[2 * v][0]
        b = total[2 * v + 1][0] if 2 * v + 1 < COMP else jnp.zeros_like(a)
        out.append(jnp.where(low, a, b) + pltpu.roll(jnp.where(low, b, a), s.W, 0))
    return out


def first_kernel(s, slots, grp, inverse_ref, *refs):
    pieces, (iterate_out, rhs_ref) = refs[:-2], refs[-2:]
    me = lax.axis_index(grp)
    if s.rows > COMP * s.W:
        rhs_ref[COMP * s.W :, :] = jnp.zeros((s.rows - COMP * s.W, LANES), jnp.float32)
    for k, piece in enumerate(pieces):
        slot = slots(me, k)
        rhs_ref[pl.ds(slot, SUBLANES, stride=s.W), :] = piece[:SUBLANES, :]
        rhs_ref[pl.ds(SUBLANES * s.W + slot, 1), :] = piece[SUBLANES:COMP, :]
    rhs = [rows_of(rhs_ref, v) for v in range(s.NV)]
    update = times(s, lambda k, i, v: rows_of(inverse_ref.at[i], v), [rhs])
    for v in range(s.NV):
        iterate_out[v * SUBLANES : (v + 1) * SUBLANES, :] = damping * update[v]


def fold_kernel(s, spread_ref, coupling_ref, out_ref):
    group = 3
    for q in range(s.Q):
        pairs = [(f, v) for f in range(FACES) for v in range(q, s.NV, s.Q)]
        for first in range(0, len(pairs), group):
            block = pairs[first : first + group]
            columns = [
                [
                    coupling_ref[(f * COMP + k) * s.rows + v * SUBLANES : (f * COMP + k) * s.rows + (v + 1) * SUBLANES, :]
                    for k in range(COMP)
                ]
                for f, v in block
            ]
            for i in range(COMP):
                acc = [None] * len(block)
                for k in range(COMP):
                    start = k * s.index_rows + q * SUBLANES
                    factor = spread_ref[i, start : start + SUBLANES, :]
                    for n in range(len(block)):
                        term = factor * columns[n][k]
                        acc[n] = term if acc[n] is None else acc[n] + term
                for n, (f, v) in enumerate(block):
                    out_ref[f, i, v * SUBLANES : (v + 1) * SUBLANES, :] = damping * acc[n]


def windows(s, table, low, high):
    if s.H == 1:
        for place, block in ((0, low), (1, high)):
            for v in range(s.NV):
                start = (v // s.Q) * 2 * s.W + place * s.W + (v % s.Q) * SUBLANES
                table[start : start + SUBLANES, :] = block[v]

        def source(v, k):
            start = (v // s.Q) * 2 * s.W + (v % s.Q) * SUBLANES + k
            return table[start : start + SUBLANES, :]

        return source
    top = s.rows + 2 * SUBLANES
    for v in range(s.NV):
        table[v * SUBLANES : (v + 1) * SUBLANES, :] = low[v]
        table[top + v * SUBLANES : top + (v + 1) * SUBLANES, :] = high[v]
    place = place_of_row(s)

    def source(v, k):
        if k == 0:
            return low[v]
        if k == s.W:
            return high[v]
        start = v * SUBLANES + k
        return jnp.where(
            place < s.W - k,
            table[start : start + SUBLANES, :],
            table[top + start - s.W : top + start - s.W + SUBLANES, :],
        )

    return source


def gathered(s, source, count, lane_ref, slot_ref):
    lane = [[lane_ref[f, q * SUBLANES : (q + 1) * SUBLANES, :] for q in range(s.Q)] for f in range(FACES)]
    slot = [[slot_ref[f, q * SUBLANES : (q + 1) * SUBLANES, :] for q in range(s.Q)] for f in range(FACES)]
    beside = [[jnp.zeros((SUBLANES, LANES), jnp.float32)] * s.NV for _ in range(FACES)]
    for k in range(count):
        here = [[slot[f][q] == k for q in range(s.Q)] for f in range(FACES)]
        for v in range(s.NV):
            tile = source(v, k)
            for f in range(FACES):
                taken = jnp.take_along_axis(tile, lane[f][v % s.Q], axis=1, mode="promise_in_bounds")
                beside[f][v] = jnp.where(here[f][v % s.Q], taken, beside[f][v])
    return beside


def own_kernel(s, folded_ref, lane_ref, slot_ref, constant_ref, iterate_ref, out_ref, table):
    own = [rows_of(iterate_ref, v) for v in range(s.NV)]
    beside = gathered(s, windows(s, table, own, own), s.W, lane_ref, slot_ref)
    coupled = times(s, lambda f, i, v: rows_of(folded_ref.at[f, i], v), beside)
    for v in range(s.NV):
        out_ref[v * SUBLANES : (v + 1) * SUBLANES, :] = (
            (1.0 - damping) * own[v] + rows_of(constant_ref, v) - coupled[v]
        )


def with_halo(s, folded_ref, lane_ref, slot_ref, even_ref, base_ref, near_ref, far_ref, table):
    even = even_ref[...] != 0
    near = [rows_of(near_ref, v) for v in range(s.NV)]
    far = [rows_of(far_ref, v) for v in range(s.NV)]
    low = [jnp.where(even, b, a) for a, b in zip(near, far)]
    high = [jnp.where(even, a, b) for a, b in zip(near, far)]
    beside = gathered(s, windows(s, table, low, high), s.W + 1, lane_ref, slot_ref)
    coupled = times(s, lambda f, i, v: rows_of(folded_ref.at[f, i], v), beside)
    return [rows_of(base_ref, v) - coupled[v] for v in range(s.NV)]


def halo_kernel(s, *refs):
    out_ref, table = refs[-2:]
    new = with_halo(s, *refs[:-2], table)
    for v in range(s.NV):
        out_ref[v * SUBLANES : (v + 1) * SUBLANES, :] = new[v]


def last_kernel(s, grp, prolongation_ref, *refs):
    out_ref, table, final = refs[-3:]
    new = with_halo(s, *refs[:-3], table)
    for v in range(s.NV):
        final[v * SUBLANES : (v + 1) * SUBLANES, :] = new[v]
    me = lax.axis_index(grp)
    rows = [final[pl.ds(j * s.W + me, 1), :] for j in range(COMP)]
    for v in range(3):
        acc = None
        for m in range(3):
            term = prolongation_ref[:, m : m + 1] * rows[3 * v + m]
            acc = term if acc is None else acc + term
        out_ref[v] = acc


def f32(*shape):
    return jax.ShapeDtypeStruct(shape, jnp.float32)


def i32(*shape):
    return jax.ShapeDtypeStruct(shape, jnp.int32)


def call(kernel, out_shape, scratch=(), flops=0):
    return pl.pallas_call(
        kernel,
        out_shape=out_shape,
        scratch_shapes=scratch,
        compiler_params=pltpu.CompilerParams(vmem_limit_bytes=16 << 20),
        cost_estimate=pl.CostEstimate(flops=flops, bytes_accessed=0, transcendentals=0),
    )


def call_loading(kernel, out_shape, operands, flops=0):
    return pl.pallas_call(
        kernel,
        out_shape=out_shape,
        in_specs=[pl.BlockSpec(memory_space=pl.ANY)] * len(operands),
        scratch_shapes=[pltpu.VMEM(x.shape, x.dtype) for x in operands]
        + [pltpu.SemaphoreType.DMA((len(operands),))],
        compiler_params=pltpu.CompilerParams(vmem_limit_bytes=16 << 20),
        cost_estimate=pl.CostEstimate(flops=flops, bytes_accessed=0, transcendentals=0),
    )(*[pltpu.with_memory_space_constraint(x, pltpu.MemorySpace.HBM) for x in operands])


def exchanges(n_dom, n_grp):
    out = []
    for first in (0, 1):
        partner = {d: d for d in range(n_dom)}
        for d in range(first, n_dom - 1, 2):
            partner[d], partner[d + 1] = d + 1, d
        perm = []
        for d in range(n_dom):
            for g in range(n_grp):
                to = g ^ 1 if partner[d] == d and n_grp % 2 == 0 else g
                perm.append((d * n_grp + g, partner[d] * n_grp + to))
        out.append(perm)
    return out


def uses_swaps(n_grp):
    return n_grp & (n_grp - 1) == 0 and n_grp <= 4


def swap_order(n_grp):
    return tuple(reversed(range(1, n_grp)))


def local(n_dom, n_grp, fine_level_residual, restriction_matrix, prolongation_matrix, block_inverse, face_coupling, neighbours):
    s = Shape(block_inverse.shape[2])
    element_width = fine_level_residual.shape[2]
    assert element_width == LANES and s.W == n_grp
    own = call_loading(restrict_kernel, f32(COMP, LANES), (fine_level_residual, restriction_matrix))
    if uses_swaps(n_grp):
        pieces = [own] + [None] * (n_grp - 1)
        for k in swap_order(n_grp):
            pieces[k] = lax.ppermute(own, "grp", [(g, g ^ k) for g in range(n_grp)])
        slots = lambda me, k: me ^ k
    else:
        all_own = lax.all_gather(own, "grp", axis=0)
        pieces = [all_own[k] for k in range(n_grp)]
        slots = lambda me, k: k
    index = i32(FACES, s.index_rows, LANES)
    inverse, spread, coupling, lane, own_slot, halo_slot, even = call_loading(
        functools.partial(prepare_kernel, s, "dom"),
        (
            f32(COMP, s.rows, LANES),
            f32(COMP, COMP * s.index_rows, LANES),
            f32(FACES * COMP * s.rows, LANES),
            index,
            index,
            index,
            i32(SUBLANES, LANES),
        ),
        (block_inverse, jnp.transpose(face_coupling, (1, 2, 0, 3)), neighbours),
        flops=10_000_000,
    )
    constant = call(
        functools.partial(first_kernel, s, slots, "grp"),
        f32(s.rows, LANES),
        (pltpu.VMEM((s.rows, LANES), jnp.float32),),
    )(inverse, *pieces)
    near_pairs, far_pairs = exchanges(n_dom, n_grp)
    table = pltpu.VMEM((s.table_rows, LANES), jnp.float32)
    iterate = constant
    for index in range(1, SWEEPS):
        far = lax.ppermute(iterate, ("dom", "grp"), far_pairs)
        near = lax.ppermute(iterate, ("dom", "grp"), near_pairs)
        if index == 1:
            folded = call(
                functools.partial(fold_kernel, s), f32(FACES, COMP, s.rows, LANES), flops=10_000_000
            )(spread, coupling)
        base = call(
            functools.partial(own_kernel, s), f32(s.rows, LANES), (table,), flops=10_000_000
        )(folded, lane, own_slot, constant, iterate)
        operands = (folded, lane, halo_slot, even, base, near, far)
        if index < SWEEPS - 1:
            iterate = call(functools.partial(halo_kernel, s), f32(s.rows, LANES), (table,))(*operands)
    return call(
        functools.partial(last_kernel, s, "grp"),
        f32(3, prolongation_matrix.shape[0], LANES),
        (table, pltpu.VMEM((s.rows, LANES), jnp.float32)),
    )(prolongation_matrix, *operands)


def solution(mesh):
    placed = (
        P(None, None, ("dom", "grp")),
        P(),
        P(),
        P(None, None, "dom"),
        P(None, None, None, "dom"),
        P(None, "dom"),
    )
    n_dom, n_grp = mesh.shape["dom"], mesh.shape["grp"]
    return jax.shard_map(
        functools.partial(local, n_dom, n_grp),
        mesh=mesh,
        in_specs=placed,
        out_specs=P(None, None, ("dom", "grp")),
        check_vma=False,
    )
```

time: 33.3 us -> 31.7 us (0.952)
  local copies, waits for them, and re-layouts: 2.58 us -> 0.1 us
  Pallas kernels: 2.92 us -> 5.38 us
  waiting for transfers between devices: 15.5 us -> 14 us
    unnamed x12 -> x3, local copies, waits for them, and re-layouts: 2.58 us -> 0.1 us
    pallas_call x8 -> x14, Pallas kernels: 2.92 us -> 5.38 us  [the longest x2 2.14 us: call_loading(): pl.pallas_call(kernel, out_shape=out_shape, in_specs=[pl.BlockSpec(memory...]
    ppermute x13, waiting for transfers between devices: 15.5 us -> 14 us  [the longest x5 11.2 us: local(): far = lax.ppermute(iterate, ('dom', 'grp'), far_pairs)]
  transfers between devices with their start and end apart: 13 -> 13, of which waited for: 8 -> 8; matrix products, arithmetic and copies ran while one was open for 4% -> 0% of each run, Pallas kernels for 0% -> 9%
where the time goes in v2:
time: 31.7 us; the launch traced here: 31.1 us
  waiting for transfers between devices  14 us (44%)
  starting transfers between devices  11.5 us (36%)
  Pallas kernels  5.38 us (17%)
    ppermute x5, waiting for transfers between devices, local(): far = lax.ppermute(iterate, ('dom', 'grp'), far_pairs)  11.2 us
    ppermute x5, starting transfers between devices, local(): near = lax.ppermute(iterate, ('dom', 'grp'), near_pairs)  5.16 us
    ppermute x3, starting transfers between devices, local(): pieces[k] = lax.ppermute(own, 'grp', [(g, g ^ k) for g in range(n_grp)])  3.35 us
    ppermute x5, starting transfers between devices, local(): far = lax.ppermute(iterate, ('dom', 'grp'), far_pairs)  3 us
    pallas_call x2, Pallas kernels, call_loading(): pl.pallas_call(kernel, out_shape=out_shape, in_specs=[pl.BlockSpec(memory...  2.14 us
    ppermute x3, waiting for transfers between devices, local(): pieces[k] = lax.ppermute(own, 'grp', [(g, g ^ k) for g in range(n_grp)])  2.07 us
    pallas_call x5, Pallas kernels, local(): call(functools.partial(own_kernel, s), f32(s.rows, LANES), (table,), flop...  1.01 us
    pallas_call x4, Pallas kernels, local(): call(functools.partial(halo_kernel, s), f32(s.rows, LANES), (table,))  0.96 us
  transfers between devices with their start and end apart: 13, of which 8 were waited for; matrix products, arithmetic and copies ran while one was open for 0% of the time, Pallas kernels for 9%

profile of v2, /device:TPU:1, one launch (start us, length us, event | category | flops | bytes accessed | tf_op | source)
XLA Modules:
  0.0 31.1 jit_solution(13296632802987492566)
XLA Ops:
  0.0 0.8 %shard_map.66.refs_0_ = f32[9,128]{1,0:T(8,128)S(1)} custom-call(f32[3,15,128]{2,1,0:T(8,128)} %residual_hbm.1, f32[3,15]{1,0:T(4,128)} %restriction_hbm.1), custom_call_target="tpu_custom_call" | custom-call | tf_op jit(solution)/shard_map/pallas_call | solution.py:285
  0.9 2.1 %collective-permute-start = (f32[9,128]{1,0:T(8,128)S(1)}, f32[9,128]{1,0:T(8,128)S(1)}, u32[]{:S(2)}, u32[]{:S(2)}) collective-permute-start(f32[9,128]{1,0:T(8,128)S(1)} %shard_map.66.refs_0_), channel_id=1, source_target_pairs={{0,1},{1,0},{2,3},{3,2},{4,5},{5,4},{6,7},{7,6},{8,9},{9,8},{10,11... | collective-permute-start | bytes 13832 | tf_op jit(solution)/shard_map/ppermute | solution.py:327
  3.0 1.2 %collective-permute-start.1 = (f32[9,128]{1,0:T(8,128)S(1)}, f32[9,128]{1,0:T(8,128)S(1)}, u32[]{:S(2)}, u32[]{:S(2)}) collective-permute-start(f32[9,128]{1,0:T(8,128)S(1)} %shard_map.66.refs_0_), channel_id=1, source_target_pairs={{0,2},{1,3},{2,0},{3,1},{4,6},{5,7},{6,4},{7,5},{8,10},{9,11},{10,... | collective-permute-start | bytes 13832 | tf_op jit(solution)/shard_map/ppermute | solution.py:327
  4.2 0.0 collective-permute-start.2
  4.2 1.3 %shard_map.64 = (f32[9,40,128]{2,1,0:T(8,128)S(1)}, f32[9,72,128]{2,1,0:T(8,128)S(1)}, f32[1080,128]{1,0:T(8,128)S(1)}, s32[3,8,128]{2,1,0:T(8,128)S(1)}, s32[3,...) custom-call(bf16[9,9,512]{2,1,0:T(8,128)(2,1)} %refs_0_.1, bf16[9,9,3,512]{3,2,1,0:T(4,128)(2,1)} %bitcast.1, ...), custom_call_target="tpu_custom_call" | custom-call | flops 10000000 | tf_op jit(solution)/shard_map/pallas_call | solution.py:285
  5.5 0.0 collective-permute-done.refs_1_
  5.5 0.0 collective-permute-done.1.refs_2_
  5.5 2.1 %collective-permute-done.2.refs_3_ = f32[9,128]{1,0:T(8,128)S(1)} collective-permute-done((f32[9,128]{1,0:T(8,128)S(1)}, f32[9,128]{1,0:T(8,128)S(1)}, u32[]{:S(2)}, u32[]{:S(2)}) %collective-permute-start.2) | collective-permute-done | bytes 4640 | tf_op jit(solution)/shard_map/ppermute | solution.py:327
  7.6 2.5 %collective-permute-start.3 = (f32[40,128]{1,0:T(8,128)S(1)}, f32[40,128]{1,0:T(8,128)S(1)}, u32[]{:S(2)}, u32[]{:S(2)}) collective-permute-start(f32[40,128]{1,0:T(8,128)S(1)} %shard_map.67.constant_ref.iterate_ref), channel_id=1, source_target_pairs={{0,4},{1,5},{2,6},{3,7},{4,0},{5,1},{6,2},{7,3},{8,12},{9,13},{10,... | collective-permute-start | bytes 61448 | tf_op jit(solution)/shard_map/ppermute | solution.py:358
  10.1 1.3 %collective-permute-start.4 = (f32[40,128]{1,0:T(8,128)S(1)}, f32[40,128]{1,0:T(8,128)S(1)}, u32[]{:S(2)}, u32[]{:S(2)}) collective-permute-start(f32[40,128]{1,0:T(8,128)S(1)} %shard_map.67.constant_ref.iterate_ref), channel_id=1, source_target_pairs={{0,1},{1,0},{2,3},{3,2},{4,8},{5,9},{6,10},{7,11},{8,4},{9,5},{10,... | collective-permute-start | bytes 61448 | tf_op jit(solution)/shard_map/ppermute | solution.py:357
  11.3 0.3 %shard_map.65.folded_ref.refs_0_ = f32[3,9,40,128]{3,2,1,0:T(8,128)S(1)} custom-call(f32[9,72,128]{2,1,0:T(8,128)S(1)} %get-tuple-element.12.spread_ref, f32[1080,128]{1,0:T(8,128)S(1)} %get-tuple-element.13.coupling_ref), custom_call_target="tpu_custom_call" | custom-call | flops 10000000 | tf_op jit(solution)/shard_map/pallas_call | solution.py:360
  11.7 0.2 shard_map.68.refs_4_
  11.9 0.0 collective-permute-done.3.refs_5_
  11.9 1.6 %collective-permute-done.4.refs_6_ = f32[40,128]{1,0:T(8,128)S(1)} collective-permute-done((f32[40,128]{1,0:T(8,128)S(1)}, f32[40,128]{1,0:T(8,128)S(1)}, u32[]{:S(2)}, u32[]{:S(2)}) %collective-permute-start.4) | collective-permute-done | bytes 20512 | tf_op jit(solution)/shard_map/ppermute | solution.py:357
  13.5 0.2 shard_map.69.iterate_ref
  13.8 0.5 %collective-permute-start.5 = (f32[40,128]{1,0:T(8,128)S(1)}, f32[40,128]{1,0:T(8,128)S(1)}, u32[]{:S(2)}, u32[]{:S(2)}) collective-permute-start(f32[40,128]{1,0:T(8,128)S(1)} %shard_map.69.iterate_ref), channel_id=1, source_target_pairs={{0,4},{1,5},{2,6},{3,7},{4,0},{5,1},{6,2},{7,3},{8,12},{9,13},{10,... | collective-permute-start | bytes 61448 | tf_op jit(solution)/shard_map/ppermute | solution.py:358
  14.3 1.0 %collective-permute-start.6 = (f32[40,128]{1,0:T(8,128)S(1)}, f32[40,128]{1,0:T(8,128)S(1)}, u32[]{:S(2)}, u32[]{:S(2)}) collective-permute-start(f32[40,128]{1,0:T(8,128)S(1)} %shard_map.69.iterate_ref), channel_id=1, source_target_pairs={{0,1},{1,0},{2,3},{3,2},{4,8},{5,9},{6,10},{7,11},{8,4},{9,5},{10,... | collective-permute-start | bytes 61448 | tf_op jit(solution)/shard_map/ppermute | solution.py:357
  15.3 0.2 shard_map.70.refs_4_
  15.5 0.0 collective-permute-done.5.refs_5_
  15.5 2.2 %collective-permute-done.6.refs_6_ = f32[40,128]{1,0:T(8,128)S(1)} collective-permute-done((f32[40,128]{1,0:T(8,128)S(1)}, f32[40,128]{1,0:T(8,128)S(1)}, u32[]{:S(2)}, u32[]{:S(2)}) %collective-permute-start.6) | collective-permute-done | bytes 20512 | tf_op jit(solution)/shard_map/ppermute | solution.py:357
  17.8 0.2 shard_map.71.iterate_ref
  18.0 0.5 %collective-permute-start.7 = (f32[40,128]{1,0:T(8,128)S(1)}, f32[40,128]{1,0:T(8,128)S(1)}, u32[]{:S(2)}, u32[]{:S(2)}) collective-permute-start(f32[40,128]{1,0:T(8,128)S(1)} %shard_map.71.iterate_ref), channel_id=1, source_target_pairs={{0,4},{1,5},{2,6},{3,7},{4,0},{5,1},{6,2},{7,3},{8,12},{9,13},{10,... | collective-permute-start | bytes 61448 | tf_op jit(solution)/shard_map/ppermute | solution.py:358
  18.5 0.5 %collective-permute-start.8 = (f32[40,128]{1,0:T(8,128)S(1)}, f32[40,128]{1,0:T(8,128)S(1)}, u32[]{:S(2)}, u32[]{:S(2)}) collective-permute-start(f32[40,128]{1,0:T(8,128)S(1)} %shard_map.71.iterate_ref), channel_id=1, source_target_pairs={{0,1},{1,0},{2,3},{3,2},{4,8},{5,9},{6,10},{7,11},{8,4},{9,5},{10,... | collective-permute-start | bytes 61448 | tf_op jit(solution)/shard_map/ppermute | solution.py:357
  18.9 0.2 shard_map.72.refs_4_
  19.1 0.2 collective-permute-done.7.refs_5_
  19.3 2.7 %collective-permute-done.8.refs_6_ = f32[40,128]{1,0:T(8,128)S(1)} collective-permute-done((f32[40,128]{1,0:T(8,128)S(1)}, f32[40,128]{1,0:T(8,128)S(1)}, u32[]{:S(2)}, u32[]{:S(2)}) %collective-permute-start.8) | collective-permute-done | bytes 20512 | tf_op jit(solution)/shard_map/ppermute | solution.py:357
  22.0 0.2 shard_map.73.iterate_ref
  22.2 0.2 collective-permute-start.10
  22.5 0.8 %collective-permute-start.9 = (f32[40,128]{1,0:T(8,128)S(1)}, f32[40,128]{1,0:T(8,128)S(1)}, u32[]{:S(2)}, u32[]{:S(2)}) collective-permute-start(f32[40,128]{1,0:T(8,128)S(1)} %shard_map.73.iterate_ref), channel_id=1, source_target_pairs={{0,4},{1,5},{2,6},{3,7},{4,0},{5,1},{6,2},{7,3},{8,12},{9,13},{10,... | collective-permute-start | bytes 61448 | tf_op jit(solution)/shard_map/ppermute | solution.py:358
  23.2 0.2 shard_map.74.refs_4_
  23.4 0.0 copy-start
  23.4 2.1 %collective-permute-done.10.refs_6_ = f32[40,128]{1,0:T(8,128)S(1)} collective-permute-done((f32[40,128]{1,0:T(8,128)S(1)}, f32[40,128]{1,0:T(8,128)S(1)}, u32[]{:S(2)}, u32[]{:S(2)}) %collective-permute-start.10) | collective-permute-done | bytes 20512 | tf_op jit(solution)/shard_map/ppermute | solution.py:357
  25.5 0.0 collective-permute-done.9.refs_5_
  25.5 0.2 shard_map.75.iterate_ref
  25.7 1.0 %collective-permute-start.11 = (f32[40,128]{1,0:T(8,128)S(1)}, f32[40,128]{1,0:T(8,128)S(1)}, u32[]{:S(2)}, u32[]{:S(2)}) collective-permute-start(f32[40,128]{1,0:T(8,128)S(1)} %shard_map.75.iterate_ref), channel_id=1, source_target_pairs={{0,4},{1,5},{2,6},{3,7},{4,0},{5,1},{6,2},{7,3},{8,12},{9,13},{10,... | collective-permute-start | bytes 61448 | tf_op jit(solution)/shard_map/ppermute | solution.py:358
  26.8 0.0 collective-permute-start.12
  26.8 0.0 copy-done
  26.8 0.1 copy.7.prolongation_ref
  26.9 0.2 shard_map.76.refs_4_
  27.1 0.5 %collective-permute-done.11.refs_5_ = f32[40,128]{1,0:T(8,128)S(1)} collective-permute-done((f32[40,128]{1,0:T(8,128)S(1)}, f32[40,128]{1,0:T(8,128)S(1)}, u32[]{:S(2)}, u32[]{:S(2)}) %collective-permute-start.11) | collective-permute-done | bytes 20512 | tf_op jit(solution)/shard_map/ppermute | solution.py:358
  27.6 2.6 %collective-permute-done.12.refs_6_ = f32[40,128]{1,0:T(8,128)S(1)} collective-permute-done((f32[40,128]{1,0:T(8,128)S(1)}, f32[40,128]{1,0:T(8,128)S(1)}, u32[]{:S(2)}, u32[]{:S(2)}) %collective-permute-start.12) | collective-permute-done | bytes 20512 | tf_op jit(solution)/shard_map/ppermute | solution.py:357
  30.2 0.9 %shard_map.77 = f32[3,15,128]{2,1,0:T(8,128)} custom-call(f32[15,3]{1,0:T(8,128)S(1)} %copy.7.prolongation_ref, f32[3,9,40,128]{3,2,1,0:T(8,128)S(1)} %shard_map.65.folded_ref.refs_0_, s32[3,8,128]{2,1,0:T(8,128)S(1)} %get-tuple-element.14.lane_ref.refs_1_, s32[3,8,128]{2,1,0:T(8,128)S(1)} %get-tuple-element.15.refs_2_, ...), custom_call_target="tpu_custom_call" | custom-call | tf_op jit(solution)/shard_map/pallas_call | solution.py:369
  (1 shorter events, 0.0 us)
Async XLA Ops:
  0.9 4.7 %collective-permute-start = (f32[9,128]{1,0:T(8,128)S(1)}, f32[9,128]{1,0:T(8,128)S(1)}, u32[]{:S(2)}, u32[]{:S(2)}) collective-permute-start(f32[9,128]{1,0:T(8,128)S(1)} %shard_map.66.refs_0_), channel_id=1, source_target_pairs={{0,1},{1,0},{2,3},{3,2},{4,5},{5,4},{6,7},{7,6},{8,9},{9,8},{10,11... | collective-permute-start | bytes 13832 | tf_op jit(solution)/shard_map/ppermute | solution.py:327
  3.0 2.6 %collective-permute-start.1 = (f32[9,128]{1,0:T(8,128)S(1)}, f32[9,128]{1,0:T(8,128)S(1)}, u32[]{:S(2)}, u32[]{:S(2)}) collective-permute-start(f32[9,128]{1,0:T(8,128)S(1)} %shard_map.66.refs_0_), channel_id=1, source_target_pairs={{0,2},{1,3},{2,0},{3,1},{4,6},{5,7},{6,4},{7,5},{8,10},{9,11},{10,... | collective-permute-start | bytes 13832 | tf_op jit(solution)/shard_map/ppermute | solution.py:327
  4.2 3.4 %collective-permute-start.2 = (f32[9,128]{1,0:T(8,128)S(1)}, f32[9,128]{1,0:T(8,128)S(1)}, u32[]{:S(2)}, u32[]{:S(2)}) collective-permute-start(f32[9,128]{1,0:T(8,128)S(1)} %shard_map.66.refs_0_), channel_id=1, source_target_pairs={{0,3},{1,2},{2,1},{3,0},{4,7},{5,6},{6,5},{7,4},{8,11},{9,10},{10,... | collective-permute-start | bytes 13832 | tf_op jit(solution)/shard_map/ppermute | solution.py:327
  7.6 4.3 %collective-permute-start.3 = (f32[40,128]{1,0:T(8,128)S(1)}, f32[40,128]{1,0:T(8,128)S(1)}, u32[]{:S(2)}, u32[]{:S(2)}) collective-permute-start(f32[40,128]{1,0:T(8,128)S(1)} %shard_map.67.constant_ref.iterate_ref), channel_id=1, source_target_pairs={{0,4},{1,5},{2,6},{3,7},{4,0},{5,1},{6,2},{7,3},{8,12},{9,13},{10,... | collective-permute-start | bytes 61448 | tf_op jit(solution)/shard_map/ppermute | solution.py:358
  10.1 3.5 %collective-permute-start.4 = (f32[40,128]{1,0:T(8,128)S(1)}, f32[40,128]{1,0:T(8,128)S(1)}, u32[]{:S(2)}, u32[]{:S(2)}) collective-permute-start(f32[40,128]{1,0:T(8,128)S(1)} %shard_map.67.constant_ref.iterate_ref), channel_id=1, source_target_pairs={{0,1},{1,0},{2,3},{3,2},{4,8},{5,9},{6,10},{7,11},{8,4},{9,5},{10,... | collective-permute-start | bytes 61448 | tf_op jit(solution)/shard_map/ppermute | solution.py:357
  13.8 1.7 %collective-permute-start.5 = (f32[40,128]{1,0:T(8,128)S(1)}, f32[40,128]{1,0:T(8,128)S(1)}, u32[]{:S(2)}, u32[]{:S(2)}) collective-permute-start(f32[40,128]{1,0:T(8,128)S(1)} %shard_map.69.iterate_ref), channel_id=1, source_target_pairs={{0,4},{1,5},{2,6},{3,7},{4,0},{5,1},{6,2},{7,3},{8,12},{9,13},{10,... | collective-permute-start | bytes 61448 | tf_op jit(solution)/shard_map/ppermute | solution.py:358
  14.3 3.5 %collective-permute-start.6 = (f32[40,128]{1,0:T(8,128)S(1)}, f32[40,128]{1,0:T(8,128)S(1)}, u32[]{:S(2)}, u32[]{:S(2)}) collective-permute-start(f32[40,128]{1,0:T(8,128)S(1)} %shard_map.69.iterate_ref), channel_id=1, source_target_pairs={{0,1},{1,0},{2,3},{3,2},{4,8},{5,9},{6,10},{7,11},{8,4},{9,5},{10,... | collective-permute-start | bytes 61448 | tf_op jit(solution)/shard_map/ppermute | solution.py:357
  18.0 1.3 %collective-permute-start.7 = (f32[40,128]{1,0:T(8,128)S(1)}, f32[40,128]{1,0:T(8,128)S(1)}, u32[]{:S(2)}, u32[]{:S(2)}) collective-permute-start(f32[40,128]{1,0:T(8,128)S(1)} %shard_map.71.iterate_ref), channel_id=1, source_target_pairs={{0,4},{1,5},{2,6},{3,7},{4,0},{5,1},{6,2},{7,3},{8,12},{9,13},{10,... | collective-permute-start | bytes 61448 | tf_op jit(solution)/shard_map/ppermute | solution.py:358
  18.5 3.5 %collective-permute-start.8 = (f32[40,128]{1,0:T(8,128)S(1)}, f32[40,128]{1,0:T(8,128)S(1)}, u32[]{:S(2)}, u32[]{:S(2)}) collective-permute-start(f32[40,128]{1,0:T(8,128)S(1)} %shard_map.71.iterate_ref), channel_id=1, source_target_pairs={{0,1},{1,0},{2,3},{3,2},{4,8},{5,9},{6,10},{7,11},{8,4},{9,5},{10,... | collective-permute-start | bytes 61448 | tf_op jit(solution)/shard_map/ppermute | solution.py:357
  22.2 3.3 %collective-permute-start.10 = (f32[40,128]{1,0:T(8,128)S(1)}, f32[40,128]{1,0:T(8,128)S(1)}, u32[]{:S(2)}, u32[]{:S(2)}) collective-permute-start(f32[40,128]{1,0:T(8,128)S(1)} %shard_map.73.iterate_ref), channel_id=1, source_target_pairs={{0,1},{1,0},{2,3},{3,2},{4,8},{5,9},{6,10},{7,11},{8,4},{9,5},{10,... | collective-permute-start | bytes 61448 | tf_op jit(solution)/shard_map/ppermute | solution.py:357
  22.5 3.0 %collective-permute-start.9 = (f32[40,128]{1,0:T(8,128)S(1)}, f32[40,128]{1,0:T(8,128)S(1)}, u32[]{:S(2)}, u32[]{:S(2)}) collective-permute-start(f32[40,128]{1,0:T(8,128)S(1)} %shard_map.73.iterate_ref), channel_id=1, source_target_pairs={{0,4},{1,5},{2,6},{3,7},{4,0},{5,1},{6,2},{7,3},{8,12},{9,13},{10,... | collective-permute-start | bytes 61448 | tf_op jit(solution)/shard_map/ppermute | solution.py:358
  23.4 3.4 %copy-start = (f32[15,3]{0,1:T(4,128)S(1)}, f32[15,3]{0,1:T(4,128)}, u32[]{:S(2)}) copy-start(f32[15,3]{0,1:T(4,128)} %param.8) | copy-start | bytes 544
  25.7 1.9 %collective-permute-start.11 = (f32[40,128]{1,0:T(8,128)S(1)}, f32[40,128]{1,0:T(8,128)S(1)}, u32[]{:S(2)}, u32[]{:S(2)}) collective-permute-start(f32[40,128]{1,0:T(8,128)S(1)} %shard_map.75.iterate_ref), channel_id=1, source_target_pairs={{0,4},{1,5},{2,6},{3,7},{4,0},{5,1},{6,2},{7,3},{8,12},{9,13},{10,... | collective-permute-start | bytes 61448 | tf_op jit(solution)/shard_map/ppermute | solution.py:358
  26.8 3.5 %collective-permute-start.12 = (f32[40,128]{1,0:T(8,128)S(1)}, f32[40,128]{1,0:T(8,128)S(1)}, u32[]{:S(2)}, u32[]{:S(2)}) collective-permute-start(f32[40,128]{1,0:T(8,128)S(1)} %shard_map.75.iterate_ref), channel_id=1, source_target_pairs={{0,1},{1,0},{2,3},{3,2},{4,8},{5,9},{6,10},{7,11},{8,4},{9,5},{10,... | collective-permute-start | bytes 61448 | tf_op jit(solution)/shard_map/ppermute | solution.py:357

commit v3 on v2

--- a/solution.py
+++ b/solution.py
@@ -207,16 +207,19 @@
 
 
 def gathered(s, source, count, lane_ref, slot_ref):
-    lane = [[lane_ref[f, q * SUBLANES : (q + 1) * SUBLANES, :] for q in range(s.Q)] for f in range(FACES)]
-    slot = [[slot_ref[f, q * SUBLANES : (q + 1) * SUBLANES, :] for q in range(s.Q)] for f in range(FACES)]
-    beside = [[jnp.zeros((SUBLANES, LANES), jnp.float32)] * s.NV for _ in range(FACES)]
-    for k in range(count):
-        here = [[slot[f][q] == k for q in range(s.Q)] for f in range(FACES)]
-        for v in range(s.NV):
-            tile = source(v, k)
-            for f in range(FACES):
-                taken = jnp.take_along_axis(tile, lane[f][v % s.Q], axis=1, mode="promise_in_bounds")
-                beside[f][v] = jnp.where(here[f][v % s.Q], taken, beside[f][v])
+    tiles = [[source(v, k) for v in range(s.NV)] for k in range(count)] if s.H > 1 else None
+    beside = []
+    for f in range(FACES):
+        lane = [lane_ref[f, q * SUBLANES : (q + 1) * SUBLANES, :] for q in range(s.Q)]
+        slot = [slot_ref[f, q * SUBLANES : (q + 1) * SUBLANES, :] for q in range(s.Q)]
+        face = [jnp.zeros((SUBLANES, LANES), jnp.float32)] * s.NV
+        for k in range(count):
+            here = [slot[q] == k for q in range(s.Q)]
+            for v in range(s.NV):
+                tile = source(v, k) if tiles is None else tiles[k][v]
+                taken = jnp.take_along_axis(tile, lane[v % s.Q], axis=1, mode="promise_in_bounds")
+                face[v] = jnp.where(here[v % s.Q], taken, face[v])
+        beside.append(face)
     return beside
 
 

time: 31.7 us -> 31.3 us (0.987)
  Pallas kernels: 5.38 us -> 4.71 us
  transfers between devices with their start and end apart: 13 -> 13, of which waited for: 8 -> 8; matrix products, arithmetic and copies ran while one was open for 0% -> 0% of each run, Pallas kernels for 9% -> 8%
where the time goes in v3:
time: 31.3 us; the launch traced here: 30.7 us
  waiting for transfers between devices  14.3 us (46%)
  starting transfers between devices  11.5 us (37%)
  Pallas kernels  4.71 us (15%)
    ppermute x5, waiting for transfers between devices, local(): far = lax.ppermute(iterate, ('dom', 'grp'), far_pairs)  11.4 us
    ppermute x5, starting transfers between devices, local(): near = lax.ppermute(iterate, ('dom', 'grp'), near_pairs)  5.16 us
    ppermute x3, starting transfers between devices, local(): pieces[k] = lax.ppermute(own, 'grp', [(g, g ^ k) for g in range(n_grp)])  3.35 us
    ppermute x5, starting transfers between devices, local(): far = lax.ppermute(iterate, ('dom', 'grp'), far_pairs)  3 us
    pallas_call x2, Pallas kernels, call_loading(): pl.pallas_call(kernel, out_shape=out_shape, in_specs=[pl.BlockSpec(memory...  2.14 us
    ppermute x3, waiting for transfers between devices, local(): pieces[k] = lax.ppermute(own, 'grp', [(g, g ^ k) for g in range(n_grp)])  2.07 us
    ppermute x5, waiting for transfers between devices, local(): near = lax.ppermute(iterate, ('dom', 'grp'), near_pairs)  0.82 us
    pallas_call x1, Pallas kernels, local(): call(functools.partial(last_kernel, s, 'grp'), f32(3, prolongation_matrix...  0.8 us
  transfers between devices with their start and end apart: 13, of which 8 were waited for; matrix products, arithmetic and copies ran while one was open for 0% of the time, Pallas kernels for 8%

profile of v3, /device:TPU:1, one launch (start us, length us, event | category | flops | bytes accessed | tf_op | source)
XLA Modules:
  0.0 30.7 jit_solution(10397051615319076006)
XLA Ops:
  0.0 0.8 %shard_map.66.refs_0_ = f32[9,128]{1,0:T(8,128)S(1)} custom-call(f32[3,15,128]{2,1,0:T(8,128)} %residual_hbm.1, f32[3,15]{1,0:T(4,128)} %restriction_hbm.1), custom_call_target="tpu_custom_call" | custom-call | tf_op jit(solution)/shard_map/pallas_call | solution.py:288
  0.9 2.1 %collective-permute-start = (f32[9,128]{1,0:T(8,128)S(1)}, f32[9,128]{1,0:T(8,128)S(1)}, u32[]{:S(2)}, u32[]{:S(2)}) collective-permute-start(f32[9,128]{1,0:T(8,128)S(1)} %shard_map.66.refs_0_), channel_id=1, source_target_pairs={{0,1},{1,0},{2,3},{3,2},{4,5},{5,4},{6,7},{7,6},{8,9},{9,8},{10,11... | collective-permute-start | bytes 13832 | tf_op jit(solution)/shard_map/ppermute | solution.py:330
  3.0 1.2 %collective-permute-start.1 = (f32[9,128]{1,0:T(8,128)S(1)}, f32[9,128]{1,0:T(8,128)S(1)}, u32[]{:S(2)}, u32[]{:S(2)}) collective-permute-start(f32[9,128]{1,0:T(8,128)S(1)} %shard_map.66.refs_0_), channel_id=1, source_target_pairs={{0,2},{1,3},{2,0},{3,1},{4,6},{5,7},{6,4},{7,5},{8,10},{9,11},{10,... | collective-permute-start | bytes 13832 | tf_op jit(solution)/shard_map/ppermute | solution.py:330
  4.2 0.0 collective-permute-start.2
  4.2 1.3 %shard_map.64 = (f32[9,40,128]{2,1,0:T(8,128)S(1)}, f32[9,72,128]{2,1,0:T(8,128)S(1)}, f32[1080,128]{1,0:T(8,128)S(1)}, s32[3,8,128]{2,1,0:T(8,128)S(1)}, s32[3,...) custom-call(bf16[9,9,512]{2,1,0:T(8,128)(2,1)} %refs_0_.1, bf16[9,9,3,512]{3,2,1,0:T(4,128)(2,1)} %bitcast.1, ...), custom_call_target="tpu_custom_call" | custom-call | flops 10000000 | tf_op jit(solution)/shard_map/pallas_call | solution.py:288
  5.5 0.0 collective-permute-done.refs_1_
  5.5 0.0 collective-permute-done.1.refs_2_
  5.5 2.1 %collective-permute-done.2.refs_3_ = f32[9,128]{1,0:T(8,128)S(1)} collective-permute-done((f32[9,128]{1,0:T(8,128)S(1)}, f32[9,128]{1,0:T(8,128)S(1)}, u32[]{:S(2)}, u32[]{:S(2)}) %collective-permute-start.2) | collective-permute-done | bytes 4640 | tf_op jit(solution)/shard_map/ppermute | solution.py:330
  7.6 2.5 %collective-permute-start.3 = (f32[40,128]{1,0:T(8,128)S(1)}, f32[40,128]{1,0:T(8,128)S(1)}, u32[]{:S(2)}, u32[]{:S(2)}) collective-permute-start(f32[40,128]{1,0:T(8,128)S(1)} %shard_map.67.constant_ref.iterate_ref), channel_id=1, source_target_pairs={{0,4},{1,5},{2,6},{3,7},{4,0},{5,1},{6,2},{7,3},{8,12},{9,13},{10,... | collective-permute-start | bytes 61448 | tf_op jit(solution)/shard_map/ppermute | solution.py:361
  10.1 1.3 %collective-permute-start.4 = (f32[40,128]{1,0:T(8,128)S(1)}, f32[40,128]{1,0:T(8,128)S(1)}, u32[]{:S(2)}, u32[]{:S(2)}) collective-permute-start(f32[40,128]{1,0:T(8,128)S(1)} %shard_map.67.constant_ref.iterate_ref), channel_id=1, source_target_pairs={{0,1},{1,0},{2,3},{3,2},{4,8},{5,9},{6,10},{7,11},{8,4},{9,5},{10,... | collective-permute-start | bytes 61448 | tf_op jit(solution)/shard_map/ppermute | solution.py:360
  11.3 0.3 %shard_map.65.folded_ref.refs_0_ = f32[3,9,40,128]{3,2,1,0:T(8,128)S(1)} custom-call(f32[9,72,128]{2,1,0:T(8,128)S(1)} %get-tuple-element.12.spread_ref, f32[1080,128]{1,0:T(8,128)S(1)} %get-tuple-element.13.coupling_ref), custom_call_target="tpu_custom_call" | custom-call | flops 10000000 | tf_op jit(solution)/shard_map/pallas_call | solution.py:363
  11.7 0.1 shard_map.68.refs_4_
  11.8 0.0 collective-permute-done.3.refs_5_
  11.9 1.7 %collective-permute-done.4.refs_6_ = f32[40,128]{1,0:T(8,128)S(1)} collective-permute-done((f32[40,128]{1,0:T(8,128)S(1)}, f32[40,128]{1,0:T(8,128)S(1)}, u32[]{:S(2)}, u32[]{:S(2)}) %collective-permute-start.4) | collective-permute-done | bytes 20512 | tf_op jit(solution)/shard_map/ppermute | solution.py:360
  13.5 0.2 shard_map.69.iterate_ref
  13.7 0.5 %collective-permute-start.5 = (f32[40,128]{1,0:T(8,128)S(1)}, f32[40,128]{1,0:T(8,128)S(1)}, u32[]{:S(2)}, u32[]{:S(2)}) collective-permute-start(f32[40,128]{1,0:T(8,128)S(1)} %shard_map.69.iterate_ref), channel_id=1, source_target_pairs={{0,4},{1,5},{2,6},{3,7},{4,0},{5,1},{6,2},{7,3},{8,12},{9,13},{10,... | collective-permute-start | bytes 61448 | tf_op jit(solution)/shard_map/ppermute | solution.py:361
  14.2 1.0 %collective-permute-start.6 = (f32[40,128]{1,0:T(8,128)S(1)}, f32[40,128]{1,0:T(8,128)S(1)}, u32[]{:S(2)}, u32[]{:S(2)}) collective-permute-start(f32[40,128]{1,0:T(8,128)S(1)} %shard_map.69.iterate_ref), channel_id=1, source_target_pairs={{0,1},{1,0},{2,3},{3,2},{4,8},{5,9},{6,10},{7,11},{8,4},{9,5},{10,... | collective-permute-start | bytes 61448 | tf_op jit(solution)/shard_map/ppermute | solution.py:360
  15.2 0.1 shard_map.70.refs_4_
  15.4 0.0 collective-permute-done.5.refs_5_
  15.4 2.3 %collective-permute-done.6.refs_6_ = f32[40,128]{1,0:T(8,128)S(1)} collective-permute-done((f32[40,128]{1,0:T(8,128)S(1)}, f32[40,128]{1,0:T(8,128)S(1)}, u32[]{:S(2)}, u32[]{:S(2)}) %collective-permute-start.6) | collective-permute-done | bytes 20512 | tf_op jit(solution)/shard_map/ppermute | solution.py:360
  17.7 0.2 shard_map.71.iterate_ref
  17.8 0.5 %collective-permute-start.7 = (f32[40,128]{1,0:T(8,128)S(1)}, f32[40,128]{1,0:T(8,128)S(1)}, u32[]{:S(2)}, u32[]{:S(2)}) collective-permute-start(f32[40,128]{1,0:T(8,128)S(1)} %shard_map.71.iterate_ref), channel_id=1, source_target_pairs={{0,4},{1,5},{2,6},{3,7},{4,0},{5,1},{6,2},{7,3},{8,12},{9,13},{10,... | collective-permute-start | bytes 61448 | tf_op jit(solution)/shard_map/ppermute | solution.py:361
  18.3 0.5 %collective-permute-start.8 = (f32[40,128]{1,0:T(8,128)S(1)}, f32[40,128]{1,0:T(8,128)S(1)}, u32[]{:S(2)}, u32[]{:S(2)}) collective-permute-start(f32[40,128]{1,0:T(8,128)S(1)} %shard_map.71.iterate_ref), channel_id=1, source_target_pairs={{0,1},{1,0},{2,3},{3,2},{4,8},{5,9},{6,10},{7,11},{8,4},{9,5},{10,... | collective-permute-start | bytes 61448 | tf_op jit(solution)/shard_map/ppermute | solution.py:360
  18.8 0.1 shard_map.72.refs_4_
  18.9 0.2 collective-permute-done.7.refs_5_
  19.2 2.7 %collective-permute-done.8.refs_6_ = f32[40,128]{1,0:T(8,128)S(1)} collective-permute-done((f32[40,128]{1,0:T(8,128)S(1)}, f32[40,128]{1,0:T(8,128)S(1)}, u32[]{:S(2)}, u32[]{:S(2)}) %collective-permute-start.8) | collective-permute-done | bytes 20512 | tf_op jit(solution)/shard_map/ppermute | solution.py:360
  21.8 0.2 shard_map.73.iterate_ref
  22.0 0.2 collective-permute-start.10
  22.2 0.8 %collective-permute-start.9 = (f32[40,128]{1,0:T(8,128)S(1)}, f32[40,128]{1,0:T(8,128)S(1)}, u32[]{:S(2)}, u32[]{:S(2)}) collective-permute-start(f32[40,128]{1,0:T(8,128)S(1)} %shard_map.73.iterate_ref), channel_id=1, source_target_pairs={{0,4},{1,5},{2,6},{3,7},{4,0},{5,1},{6,2},{7,3},{8,12},{9,13},{10,... | collective-permute-start | bytes 61448 | tf_op jit(solution)/shard_map/ppermute | solution.py:361
  23.0 0.1 shard_map.74.refs_4_
  23.1 0.0 copy-start
  23.1 2.1 %collective-permute-done.10.refs_6_ = f32[40,128]{1,0:T(8,128)S(1)} collective-permute-done((f32[40,128]{1,0:T(8,128)S(1)}, f32[40,128]{1,0:T(8,128)S(1)}, u32[]{:S(2)}, u32[]{:S(2)}) %collective-permute-start.10) | collective-permute-done | bytes 20512 | tf_op jit(solution)/shard_map/ppermute | solution.py:360
  25.3 0.0 collective-permute-done.9.refs_5_
  25.3 0.2 shard_map.75.iterate_ref
  25.4 1.0 %collective-permute-start.11 = (f32[40,128]{1,0:T(8,128)S(1)}, f32[40,128]{1,0:T(8,128)S(1)}, u32[]{:S(2)}, u32[]{:S(2)}) collective-permute-start(f32[40,128]{1,0:T(8,128)S(1)} %shard_map.75.iterate_ref), channel_id=1, source_target_pairs={{0,4},{1,5},{2,6},{3,7},{4,0},{5,1},{6,2},{7,3},{8,12},{9,13},{10,... | collective-permute-start | bytes 61448 | tf_op jit(solution)/shard_map/ppermute | solution.py:361
  26.5 0.0 collective-permute-start.12
  26.5 0.0 copy-done
  26.5 0.1 copy.7.prolongation_ref
  26.6 0.1 shard_map.76.refs_4_
  26.7 0.6 %collective-permute-done.11.refs_5_ = f32[40,128]{1,0:T(8,128)S(1)} collective-permute-done((f32[40,128]{1,0:T(8,128)S(1)}, f32[40,128]{1,0:T(8,128)S(1)}, u32[]{:S(2)}, u32[]{:S(2)}) %collective-permute-start.11) | collective-permute-done | bytes 20512 | tf_op jit(solution)/shard_map/ppermute | solution.py:361
  27.3 2.6 %collective-permute-done.12.refs_6_ = f32[40,128]{1,0:T(8,128)S(1)} collective-permute-done((f32[40,128]{1,0:T(8,128)S(1)}, f32[40,128]{1,0:T(8,128)S(1)}, u32[]{:S(2)}, u32[]{:S(2)}) %collective-permute-start.12) | collective-permute-done | bytes 20512 | tf_op jit(solution)/shard_map/ppermute | solution.py:360
  29.9 0.8 %shard_map.77 = f32[3,15,128]{2,1,0:T(8,128)} custom-call(f32[15,3]{1,0:T(8,128)S(1)} %copy.7.prolongation_ref, f32[3,9,40,128]{3,2,1,0:T(8,128)S(1)} %shard_map.65.folded_ref.refs_0_, s32[3,8,128]{2,1,0:T(8,128)S(1)} %get-tuple-element.14.lane_ref.refs_1_, s32[3,8,128]{2,1,0:T(8,128)S(1)} %get-tuple-element.15.refs_2_, ...), custom_call_target="tpu_custom_call" | custom-call | tf_op jit(solution)/shard_map/pallas_call | solution.py:372
  (1 shorter events, 0.0 us)
Async XLA Ops:
  0.9 4.7 %collective-permute-start = (f32[9,128]{1,0:T(8,128)S(1)}, f32[9,128]{1,0:T(8,128)S(1)}, u32[]{:S(2)}, u32[]{:S(2)}) collective-permute-start(f32[9,128]{1,0:T(8,128)S(1)} %shard_map.66.refs_0_), channel_id=1, source_target_pairs={{0,1},{1,0},{2,3},{3,2},{4,5},{5,4},{6,7},{7,6},{8,9},{9,8},{10,11... | collective-permute-start | bytes 13832 | tf_op jit(solution)/shard_map/ppermute | solution.py:330
  3.0 2.6 %collective-permute-start.1 = (f32[9,128]{1,0:T(8,128)S(1)}, f32[9,128]{1,0:T(8,128)S(1)}, u32[]{:S(2)}, u32[]{:S(2)}) collective-permute-start(f32[9,128]{1,0:T(8,128)S(1)} %shard_map.66.refs_0_), channel_id=1, source_target_pairs={{0,2},{1,3},{2,0},{3,1},{4,6},{5,7},{6,4},{7,5},{8,10},{9,11},{10,... | collective-permute-start | bytes 13832 | tf_op jit(solution)/shard_map/ppermute | solution.py:330
  4.2 3.4 %collective-permute-start.2 = (f32[9,128]{1,0:T(8,128)S(1)}, f32[9,128]{1,0:T(8,128)S(1)}, u32[]{:S(2)}, u32[]{:S(2)}) collective-permute-start(f32[9,128]{1,0:T(8,128)S(1)} %shard_map.66.refs_0_), channel_id=1, source_target_pairs={{0,3},{1,2},{2,1},{3,0},{4,7},{5,6},{6,5},{7,4},{8,11},{9,10},{10,... | collective-permute-start | bytes 13832 | tf_op jit(solution)/shard_map/ppermute | solution.py:330
  7.6 4.2 %collective-permute-start.3 = (f32[40,128]{1,0:T(8,128)S(1)}, f32[40,128]{1,0:T(8,128)S(1)}, u32[]{:S(2)}, u32[]{:S(2)}) collective-permute-start(f32[40,128]{1,0:T(8,128)S(1)} %shard_map.67.constant_ref.iterate_ref), channel_id=1, source_target_pairs={{0,4},{1,5},{2,6},{3,7},{4,0},{5,1},{6,2},{7,3},{8,12},{9,13},{10,... | collective-permute-start | bytes 61448 | tf_op jit(solution)/shard_map/ppermute | solution.py:361
  10.1 3.5 %collective-permute-start.4 = (f32[40,128]{1,0:T(8,128)S(1)}, f32[40,128]{1,0:T(8,128)S(1)}, u32[]{:S(2)}, u32[]{:S(2)}) collective-permute-start(f32[40,128]{1,0:T(8,128)S(1)} %shard_map.67.constant_ref.iterate_ref), channel_id=1, source_target_pairs={{0,1},{1,0},{2,3},{3,2},{4,8},{5,9},{6,10},{7,11},{8,4},{9,5},{10,... | collective-permute-start | bytes 61448 | tf_op jit(solution)/shard_map/ppermute | solution.py:360
  13.7 1.7 %collective-permute-start.5 = (f32[40,128]{1,0:T(8,128)S(1)}, f32[40,128]{1,0:T(8,128)S(1)}, u32[]{:S(2)}, u32[]{:S(2)}) collective-permute-start(f32[40,128]{1,0:T(8,128)S(1)} %shard_map.69.iterate_ref), channel_id=1, source_target_pairs={{0,4},{1,5},{2,6},{3,7},{4,0},{5,1},{6,2},{7,3},{8,12},{9,13},{10,... | collective-permute-start | bytes 61448 | tf_op jit(solution)/shard_map/ppermute | solution.py:361
  14.2 3.5 %collective-permute-start.6 = (f32[40,128]{1,0:T(8,128)S(1)}, f32[40,128]{1,0:T(8,128)S(1)}, u32[]{:S(2)}, u32[]{:S(2)}) collective-permute-start(f32[40,128]{1,0:T(8,128)S(1)} %shard_map.69.iterate_ref), channel_id=1, source_target_pairs={{0,1},{1,0},{2,3},{3,2},{4,8},{5,9},{6,10},{7,11},{8,4},{9,5},{10,... | collective-permute-start | bytes 61448 | tf_op jit(solution)/shard_map/ppermute | solution.py:360
  17.8 1.3 %collective-permute-start.7 = (f32[40,128]{1,0:T(8,128)S(1)}, f32[40,128]{1,0:T(8,128)S(1)}, u32[]{:S(2)}, u32[]{:S(2)}) collective-permute-start(f32[40,128]{1,0:T(8,128)S(1)} %shard_map.71.iterate_ref), channel_id=1, source_target_pairs={{0,4},{1,5},{2,6},{3,7},{4,0},{5,1},{6,2},{7,3},{8,12},{9,13},{10,... | collective-permute-start | bytes 61448 | tf_op jit(solution)/shard_map/ppermute | solution.py:361
  18.3 3.5 %collective-permute-start.8 = (f32[40,128]{1,0:T(8,128)S(1)}, f32[40,128]{1,0:T(8,128)S(1)}, u32[]{:S(2)}, u32[]{:S(2)}) collective-permute-start(f32[40,128]{1,0:T(8,128)S(1)} %shard_map.71.iterate_ref), channel_id=1, source_target_pairs={{0,1},{1,0},{2,3},{3,2},{4,8},{5,9},{6,10},{7,11},{8,4},{9,5},{10,... | collective-permute-start | bytes 61448 | tf_op jit(solution)/shard_map/ppermute | solution.py:360
  22.0 3.3 %collective-permute-start.10 = (f32[40,128]{1,0:T(8,128)S(1)}, f32[40,128]{1,0:T(8,128)S(1)}, u32[]{:S(2)}, u32[]{:S(2)}) collective-permute-start(f32[40,128]{1,0:T(8,128)S(1)} %shard_map.73.iterate_ref), channel_id=1, source_target_pairs={{0,1},{1,0},{2,3},{3,2},{4,8},{5,9},{6,10},{7,11},{8,4},{9,5},{10,... | collective-permute-start | bytes 61448 | tf_op jit(solution)/shard_map/ppermute | solution.py:360
  22.2 3.0 %collective-permute-start.9 = (f32[40,128]{1,0:T(8,128)S(1)}, f32[40,128]{1,0:T(8,128)S(1)}, u32[]{:S(2)}, u32[]{:S(2)}) collective-permute-start(f32[40,128]{1,0:T(8,128)S(1)} %shard_map.73.iterate_ref), channel_id=1, source_target_pairs={{0,4},{1,5},{2,6},{3,7},{4,0},{5,1},{6,2},{7,3},{8,12},{9,13},{10,... | collective-permute-start | bytes 61448 | tf_op jit(solution)/shard_map/ppermute | solution.py:361
  23.1 3.3 %copy-start = (f32[15,3]{0,1:T(4,128)S(1)}, f32[15,3]{0,1:T(4,128)}, u32[]{:S(2)}) copy-start(f32[15,3]{0,1:T(4,128)} %param.8) | copy-start | bytes 544
  25.4 1.9 %collective-permute-start.11 = (f32[40,128]{1,0:T(8,128)S(1)}, f32[40,128]{1,0:T(8,128)S(1)}, u32[]{:S(2)}, u32[]{:S(2)}) collective-permute-start(f32[40,128]{1,0:T(8,128)S(1)} %shard_map.75.iterate_ref), channel_id=1, source_target_pairs={{0,4},{1,5},{2,6},{3,7},{4,0},{5,1},{6,2},{7,3},{8,12},{9,13},{10,... | collective-permute-start | bytes 61448 | tf_op jit(solution)/shard_map/ppermute | solution.py:361
  26.5 3.5 %collective-permute-start.12 = (f32[40,128]{1,0:T(8,128)S(1)}, f32[40,128]{1,0:T(8,128)S(1)}, u32[]{:S(2)}, u32[]{:S(2)}) collective-permute-start(f32[40,128]{1,0:T(8,128)S(1)} %shard_map.75.iterate_ref), channel_id=1, source_target_pairs={{0,1},{1,0},{2,3},{3,2},{4,8},{5,9},{6,10},{7,11},{8,4},{9,5},{10,... | collective-permute-start | bytes 61448 | tf_op jit(solution)/shard_map/ppermute | solution.py:360

commit v4 on v3

--- a/solution.py
+++ b/solution.py
@@ -296,7 +296,7 @@
     )(*[pltpu.with_memory_space_constraint(x, pltpu.MemorySpace.HBM) for x in operands])
 
 
-def exchanges(n_dom, n_grp):
+def exchanges(n_dom, n_grp, fill):
     out = []
     for first in (0, 1):
         partner = {d: d for d in range(n_dom)}
@@ -306,7 +306,8 @@
         for d in range(n_dom):
             for g in range(n_grp):
                 to = g ^ 1 if partner[d] == d and n_grp % 2 == 0 else g
-                perm.append((d * n_grp + g, partner[d] * n_grp + to))
+                if fill or partner[d] != d:
+                    perm.append((d * n_grp + g, partner[d] * n_grp + to))
         out.append(perm)
     return out
 
@@ -353,10 +354,10 @@
         f32(s.rows, LANES),
         (pltpu.VMEM((s.rows, LANES), jnp.float32),),
     )(inverse, *pieces)
-    near_pairs, far_pairs = exchanges(n_dom, n_grp)
     table = pltpu.VMEM((s.table_rows, LANES), jnp.float32)
     iterate = constant
     for index in range(1, SWEEPS):
+        near_pairs, far_pairs = exchanges(n_dom, n_grp, index < SWEEPS - 1)
         far = lax.ppermute(iterate, ("dom", "grp"), far_pairs)
         near = lax.ppermute(iterate, ("dom", "grp"), near_pairs)
         if index == 1:

time: 31.3 us -> 32.5 us (1.038); the launches traced: 30.7 us -> 32.4 us
  starting transfers between devices: 11.5 us -> 13.4 us
    ppermute x5, starting transfers between devices: 3 us -> 4.91 us  [local(): far = lax.ppermute(iterate, ('dom', 'grp'), far_pairs)]
    ppermute x5, waiting for transfers between devices: 0.82 us -> 0.23 us  [local(): near = lax.ppermute(iterate, ('dom', 'grp'), near_pairs)]
  transfers between devices with their start and end apart: 13 -> 13, of which waited for: 8 -> 7; matrix products, arithmetic and copies ran while one was open for 0% -> 0% of each run, Pallas kernels for 8% -> 7%
where the time goes in v4:
time: 32.5 us; the launch traced here: 32.4 us
  waiting for transfers between devices  14 us (43%)
  starting transfers between devices  13.4 us (41%)
  Pallas kernels  4.71 us (14%)
    ppermute x5, waiting for transfers between devices, local(): far = lax.ppermute(iterate, ('dom', 'grp'), far_pairs)  11.7 us
    ppermute x5, starting transfers between devices, local(): near = lax.ppermute(iterate, ('dom', 'grp'), near_pairs)  5.16 us
    ppermute x5, starting transfers between devices, local(): far = lax.ppermute(iterate, ('dom', 'grp'), far_pairs)  4.91 us
    ppermute x3, starting transfers between devices, local(): pieces[k] = lax.ppermute(own, 'grp', [(g, g ^ k) for g in range(n_grp)])  3.35 us
    pallas_call x2, Pallas kernels, call_loading(): pl.pallas_call(kernel, out_shape=out_shape, in_specs=[pl.BlockSpec(memory...  2.14 us
    ppermute x3, waiting for transfers between devices, local(): pieces[k] = lax.ppermute(own, 'grp', [(g, g ^ k) for g in range(n_grp)])  2.07 us
    pallas_call x1, Pallas kernels, local(): call(functools.partial(last_kernel, s, 'grp'), f32(3, prolongation_matrix...  0.8 us
    pallas_call x5, Pallas kernels, local(): call(functools.partial(own_kernel, s), f32(s.rows, LANES), (table,), flop...  0.74 us
  transfers between devices with their start and end apart: 13, of which 7 were waited for; matrix products, arithmetic and copies ran while one was open for 0% of the time, Pallas kernels for 7%

profile of v4, /device:TPU:1, one launch (start us, length us, event | category | flops | bytes accessed | tf_op | source)
XLA Modules:
  0.0 32.4 jit_solution(14455913094391492252)
XLA Ops:
  0.0 0.8 %shard_map.66.refs_0_ = f32[9,128]{1,0:T(8,128)S(1)} custom-call(f32[3,15,128]{2,1,0:T(8,128)} %residual_hbm.1, f32[3,15]{1,0:T(4,128)} %restriction_hbm.1), custom_call_target="tpu_custom_call" | custom-call | tf_op jit(solution)/shard_map/pallas_call | solution.py:288
  0.9 2.1 %collective-permute-start = (f32[9,128]{1,0:T(8,128)S(1)}, f32[9,128]{1,0:T(8,128)S(1)}, u32[]{:S(2)}, u32[]{:S(2)}) collective-permute-start(f32[9,128]{1,0:T(8,128)S(1)} %shard_map.66.refs_0_), channel_id=1, source_target_pairs={{0,1},{1,0},{2,3},{3,2},{4,5},{5,4},{6,7},{7,6},{8,9},{9,8},{10,11... | collective-permute-start | bytes 13832 | tf_op jit(solution)/shard_map/ppermute | solution.py:331
  3.0 1.2 %collective-permute-start.1 = (f32[9,128]{1,0:T(8,128)S(1)}, f32[9,128]{1,0:T(8,128)S(1)}, u32[]{:S(2)}, u32[]{:S(2)}) collective-permute-start(f32[9,128]{1,0:T(8,128)S(1)} %shard_map.66.refs_0_), channel_id=1, source_target_pairs={{0,2},{1,3},{2,0},{3,1},{4,6},{5,7},{6,4},{7,5},{8,10},{9,11},{10,... | collective-permute-start | bytes 13832 | tf_op jit(solution)/shard_map/ppermute | solution.py:331
  4.2 0.0 collective-permute-start.2
  4.2 1.3 %shard_map.64 = (f32[9,40,128]{2,1,0:T(8,128)S(1)}, f32[9,72,128]{2,1,0:T(8,128)S(1)}, f32[1080,128]{1,0:T(8,128)S(1)}, s32[3,8,128]{2,1,0:T(8,128)S(1)}, s32[3,...) custom-call(bf16[9,9,512]{2,1,0:T(8,128)(2,1)} %refs_0_.1, bf16[9,9,3,512]{3,2,1,0:T(4,128)(2,1)} %bitcast.1, ...), custom_call_target="tpu_custom_call" | custom-call | flops 10000000 | tf_op jit(solution)/shard_map/pallas_call | solution.py:288
  5.5 0.0 collective-permute-done.refs_1_
  5.5 0.0 collective-permute-done.1.refs_2_
  5.5 2.1 %collective-permute-done.2.refs_3_ = f32[9,128]{1,0:T(8,128)S(1)} collective-permute-done((f32[9,128]{1,0:T(8,128)S(1)}, f32[9,128]{1,0:T(8,128)S(1)}, u32[]{:S(2)}, u32[]{:S(2)}) %collective-permute-start.2) | collective-permute-done | bytes 4640 | tf_op jit(solution)/shard_map/ppermute | solution.py:331
  7.6 2.5 %collective-permute-start.3 = (f32[40,128]{1,0:T(8,128)S(1)}, f32[40,128]{1,0:T(8,128)S(1)}, u32[]{:S(2)}, u32[]{:S(2)}) collective-permute-start(f32[40,128]{1,0:T(8,128)S(1)} %shard_map.67.constant_ref.iterate_ref), channel_id=1, source_target_pairs={{0,4},{1,5},{2,6},{3,7},{4,0},{5,1},{6,2},{7,3},{8,12},{9,13},{10,... | collective-permute-start | bytes 61448 | tf_op jit(solution)/shard_map/ppermute | solution.py:362
  10.1 1.3 %collective-permute-start.4 = (f32[40,128]{1,0:T(8,128)S(1)}, f32[40,128]{1,0:T(8,128)S(1)}, u32[]{:S(2)}, u32[]{:S(2)}) collective-permute-start(f32[40,128]{1,0:T(8,128)S(1)} %shard_map.67.constant_ref.iterate_ref), channel_id=1, source_target_pairs={{0,1},{1,0},{2,3},{3,2},{4,8},{5,9},{6,10},{7,11},{8,4},{9,5},{10,... | collective-permute-start | bytes 61448 | tf_op jit(solution)/shard_map/ppermute | solution.py:361
  11.3 0.3 %shard_map.65.folded_ref.refs_0_ = f32[3,9,40,128]{3,2,1,0:T(8,128)S(1)} custom-call(f32[9,72,128]{2,1,0:T(8,128)S(1)} %get-tuple-element.12.spread_ref, f32[1080,128]{1,0:T(8,128)S(1)} %get-tuple-element.13.coupling_ref), custom_call_target="tpu_custom_call" | custom-call | flops 10000000 | tf_op jit(solution)/shard_map/pallas_call | solution.py:364
  11.7 0.1 shard_map.68.refs_4_
  11.8 0.0 collective-permute-done.3.refs_5_
  11.9 1.7 %collective-permute-done.4.refs_6_ = f32[40,128]{1,0:T(8,128)S(1)} collective-permute-done((f32[40,128]{1,0:T(8,128)S(1)}, f32[40,128]{1,0:T(8,128)S(1)}, u32[]{:S(2)}, u32[]{:S(2)}) %collective-permute-start.4) | collective-permute-done | bytes 20512 | tf_op jit(solution)/shard_map/ppermute | solution.py:361
  13.5 0.2 shard_map.69.iterate_ref
  13.7 0.5 %collective-permute-start.5 = (f32[40,128]{1,0:T(8,128)S(1)}, f32[40,128]{1,0:T(8,128)S(1)}, u32[]{:S(2)}, u32[]{:S(2)}) collective-permute-start(f32[40,128]{1,0:T(8,128)S(1)} %shard_map.69.iterate_ref), channel_id=1, source_target_pairs={{0,4},{1,5},{2,6},{3,7},{4,0},{5,1},{6,2},{7,3},{8,12},{9,13},{10,... | collective-permute-start | bytes 61448 | tf_op jit(solution)/shard_map/ppermute | solution.py:362
  14.2 1.0 %collective-permute-start.6 = (f32[40,128]{1,0:T(8,128)S(1)}, f32[40,128]{1,0:T(8,128)S(1)}, u32[]{:S(2)}, u32[]{:S(2)}) collective-permute-start(f32[40,128]{1,0:T(8,128)S(1)} %shard_map.69.iterate_ref), channel_id=1, source_target_pairs={{0,1},{1,0},{2,3},{3,2},{4,8},{5,9},{6,10},{7,11},{8,4},{9,5},{10,... | collective-permute-start | bytes 61448 | tf_op jit(solution)/shard_map/ppermute | solution.py:361
  15.2 0.1 shard_map.70.refs_4_
  15.4 0.0 collective-permute-done.5.refs_5_
  15.4 2.3 %collective-permute-done.6.refs_6_ = f32[40,128]{1,0:T(8,128)S(1)} collective-permute-done((f32[40,128]{1,0:T(8,128)S(1)}, f32[40,128]{1,0:T(8,128)S(1)}, u32[]{:S(2)}, u32[]{:S(2)}) %collective-permute-start.6) | collective-permute-done | bytes 20512 | tf_op jit(solution)/shard_map/ppermute | solution.py:361
  17.7 0.2 shard_map.71.iterate_ref
  17.8 0.5 %collective-permute-start.7 = (f32[40,128]{1,0:T(8,128)S(1)}, f32[40,128]{1,0:T(8,128)S(1)}, u32[]{:S(2)}, u32[]{:S(2)}) collective-permute-start(f32[40,128]{1,0:T(8,128)S(1)} %shard_map.71.iterate_ref), channel_id=1, source_target_pairs={{0,4},{1,5},{2,6},{3,7},{4,0},{5,1},{6,2},{7,3},{8,12},{9,13},{10,... | collective-permute-start | bytes 61448 | tf_op jit(solution)/shard_map/ppermute | solution.py:362
  18.3 0.5 %collective-permute-start.8 = (f32[40,128]{1,0:T(8,128)S(1)}, f32[40,128]{1,0:T(8,128)S(1)}, u32[]{:S(2)}, u32[]{:S(2)}) collective-permute-start(f32[40,128]{1,0:T(8,128)S(1)} %shard_map.71.iterate_ref), channel_id=1, source_target_pairs={{0,1},{1,0},{2,3},{3,2},{4,8},{5,9},{6,10},{7,11},{8,4},{9,5},{10,... | collective-permute-start | bytes 61448 | tf_op jit(solution)/shard_map/ppermute | solution.py:361
  18.8 0.1 shard_map.72.refs_4_
  18.9 0.2 collective-permute-done.7.refs_5_
  19.2 2.7 %collective-permute-done.8.refs_6_ = f32[40,128]{1,0:T(8,128)S(1)} collective-permute-done((f32[40,128]{1,0:T(8,128)S(1)}, f32[40,128]{1,0:T(8,128)S(1)}, u32[]{:S(2)}, u32[]{:S(2)}) %collective-permute-start.8) | collective-permute-done | bytes 20512 | tf_op jit(solution)/shard_map/ppermute | solution.py:361
  21.8 0.2 shard_map.73.iterate_ref
  22.0 0.2 collective-permute-start.10
  22.2 0.8 %collective-permute-start.9 = (f32[40,128]{1,0:T(8,128)S(1)}, f32[40,128]{1,0:T(8,128)S(1)}, u32[]{:S(2)}, u32[]{:S(2)}) collective-permute-start(f32[40,128]{1,0:T(8,128)S(1)} %shard_map.73.iterate_ref), channel_id=1, source_target_pairs={{0,4},{1,5},{2,6},{3,7},{4,0},{5,1},{6,2},{7,3},{8,12},{9,13},{10,... | collective-permute-start | bytes 61448 | tf_op jit(solution)/shard_map/ppermute | solution.py:362
  23.0 0.1 shard_map.74.refs_4_
  23.1 0.0 copy-start
  23.1 2.1 %collective-permute-done.10.refs_6_ = f32[40,128]{1,0:T(8,128)S(1)} collective-permute-done((f32[40,128]{1,0:T(8,128)S(1)}, f32[40,128]{1,0:T(8,128)S(1)}, u32[]{:S(2)}, u32[]{:S(2)}) %collective-permute-start.10) | collective-permute-done | bytes 20512 | tf_op jit(solution)/shard_map/ppermute | solution.py:361
  25.3 0.0 collective-permute-done.9.refs_5_
  25.3 0.2 shard_map.75.iterate_ref
  25.4 1.0 %collective-permute-start.11 = (f32[40,128]{1,0:T(8,128)S(1)}, f32[40,128]{1,0:T(8,128)S(1)}, u32[]{:S(2)}, u32[]{:S(2)}) collective-permute-start(f32[40,128]{1,0:T(8,128)S(1)} %shard_map.75.iterate_ref), channel_id=1, source_target_pairs={{0,4},{1,5},{2,6},{3,7},{4,0},{5,1},{6,2},{7,3},{8,12},{9,13},{10,... | collective-permute-start | bytes 61448 | tf_op jit(solution)/shard_map/ppermute | solution.py:362
  26.5 1.9 %collective-permute-start.12 = (f32[40,128]{1,0:T(8,128)S(1)}, f32[40,128]{1,0:T(8,128)S(1)}, u32[]{:S(2)}, u32[]{:S(2)}) collective-permute-start(f32[40,128]{1,0:T(8,128)S(1)} %shard_map.75.iterate_ref), channel_id=1, source_target_pairs={{4,8},{5,9},{6,10},{7,11},{8,4},{9,5},{10,6},{11,7},{12,16},{13,17... | collective-permute-start | bytes 61448 | tf_op jit(solution)/shard_map/ppermute | solution.py:361
  28.4 0.0 copy-done
  28.4 0.1 copy.7.prolongation_ref
  28.5 0.1 shard_map.76.refs_4_
  28.6 0.0 collective-permute-done.11.refs_5_
  28.7 2.9 %collective-permute-done.12.refs_6_ = f32[40,128]{1,0:T(8,128)S(1)} collective-permute-done((f32[40,128]{1,0:T(8,128)S(1)}, f32[40,128]{1,0:T(8,128)S(1)}, u32[]{:S(2)}, u32[]{:S(2)}) %collective-permute-start.12) | collective-permute-done | bytes 20512 | tf_op jit(solution)/shard_map/ppermute | solution.py:361
  31.6 0.8 %shard_map.77 = f32[3,15,128]{2,1,0:T(8,128)} custom-call(f32[15,3]{1,0:T(8,128)S(1)} %copy.7.prolongation_ref, f32[3,9,40,128]{3,2,1,0:T(8,128)S(1)} %shard_map.65.folded_ref.refs_0_, s32[3,8,128]{2,1,0:T(8,128)S(1)} %get-tuple-element.14.lane_ref.refs_1_, s32[3,8,128]{2,1,0:T(8,128)S(1)} %get-tuple-element.15.refs_2_, ...), custom_call_target="tpu_custom_call" | custom-call | tf_op jit(solution)/shard_map/pallas_call | solution.py:373
  (1 shorter events, 0.0 us)
Async XLA Ops:
  0.9 4.7 %collective-permute-start = (f32[9,128]{1,0:T(8,128)S(1)}, f32[9,128]{1,0:T(8,128)S(1)}, u32[]{:S(2)}, u32[]{:S(2)}) collective-permute-start(f32[9,128]{1,0:T(8,128)S(1)} %shard_map.66.refs_0_), channel_id=1, source_target_pairs={{0,1},{1,0},{2,3},{3,2},{4,5},{5,4},{6,7},{7,6},{8,9},{9,8},{10,11... | collective-permute-start | bytes 13832 | tf_op jit(solution)/shard_map/ppermute | solution.py:331
  3.0 2.6 %collective-permute-start.1 = (f32[9,128]{1,0:T(8,128)S(1)}, f32[9,128]{1,0:T(8,128)S(1)}, u32[]{:S(2)}, u32[]{:S(2)}) collective-permute-start(f32[9,128]{1,0:T(8,128)S(1)} %shard_map.66.refs_0_), channel_id=1, source_target_pairs={{0,2},{1,3},{2,0},{3,1},{4,6},{5,7},{6,4},{7,5},{8,10},{9,11},{10,... | collective-permute-start | bytes 13832 | tf_op jit(solution)/shard_map/ppermute | solution.py:331
  4.2 3.4 %collective-permute-start.2 = (f32[9,128]{1,0:T(8,128)S(1)}, f32[9,128]{1,0:T(8,128)S(1)}, u32[]{:S(2)}, u32[]{:S(2)}) collective-permute-start(f32[9,128]{1,0:T(8,128)S(1)} %shard_map.66.refs_0_), channel_id=1, source_target_pairs={{0,3},{1,2},{2,1},{3,0},{4,7},{5,6},{6,5},{7,4},{8,11},{9,10},{10,... | collective-permute-start | bytes 13832 | tf_op jit(solution)/shard_map/ppermute | solution.py:331
  7.6 4.2 %collective-permute-start.3 = (f32[40,128]{1,0:T(8,128)S(1)}, f32[40,128]{1,0:T(8,128)S(1)}, u32[]{:S(2)}, u32[]{:S(2)}) collective-permute-start(f32[40,128]{1,0:T(8,128)S(1)} %shard_map.67.constant_ref.iterate_ref), channel_id=1, source_target_pairs={{0,4},{1,5},{2,6},{3,7},{4,0},{5,1},{6,2},{7,3},{8,12},{9,13},{10,... | collective-permute-start | bytes 61448 | tf_op jit(solution)/shard_map/ppermute | solution.py:362
  10.1 3.5 %collective-permute-start.4 = (f32[40,128]{1,0:T(8,128)S(1)}, f32[40,128]{1,0:T(8,128)S(1)}, u32[]{:S(2)}, u32[]{:S(2)}) collective-permute-start(f32[40,128]{1,0:T(8,128)S(1)} %shard_map.67.constant_ref.iterate_ref), channel_id=1, source_target_pairs={{0,1},{1,0},{2,3},{3,2},{4,8},{5,9},{6,10},{7,11},{8,4},{9,5},{10,... | collective-permute-start | bytes 61448 | tf_op jit(solution)/shard_map/ppermute | solution.py:361
  13.7 1.7 %collective-permute-start.5 = (f32[40,128]{1,0:T(8,128)S(1)}, f32[40,128]{1,0:T(8,128)S(1)}, u32[]{:S(2)}, u32[]{:S(2)}) collective-permute-start(f32[40,128]{1,0:T(8,128)S(1)} %shard_map.69.iterate_ref), channel_id=1, source_target_pairs={{0,4},{1,5},{2,6},{3,7},{4,0},{5,1},{6,2},{7,3},{8,12},{9,13},{10,... | collective-permute-start | bytes 61448 | tf_op jit(solution)/shard_map/ppermute | solution.py:362
  14.2 3.5 %collective-permute-start.6 = (f32[40,128]{1,0:T(8,128)S(1)}, f32[40,128]{1,0:T(8,128)S(1)}, u32[]{:S(2)}, u32[]{:S(2)}) collective-permute-start(f32[40,128]{1,0:T(8,128)S(1)} %shard_map.69.iterate_ref), channel_id=1, source_target_pairs={{0,1},{1,0},{2,3},{3,2},{4,8},{5,9},{6,10},{7,11},{8,4},{9,5},{10,... | collective-permute-start | bytes 61448 | tf_op jit(solution)/shard_map/ppermute | solution.py:361
  17.8 1.3 %collective-permute-start.7 = (f32[40,128]{1,0:T(8,128)S(1)}, f32[40,128]{1,0:T(8,128)S(1)}, u32[]{:S(2)}, u32[]{:S(2)}) collective-permute-start(f32[40,128]{1,0:T(8,128)S(1)} %shard_map.71.iterate_ref), channel_id=1, source_target_pairs={{0,4},{1,5},{2,6},{3,7},{4,0},{5,1},{6,2},{7,3},{8,12},{9,13},{10,... | collective-permute-start | bytes 61448 | tf_op jit(solution)/shard_map/ppermute | solution.py:362
  18.3 3.5 %collective-permute-start.8 = (f32[40,128]{1,0:T(8,128)S(1)}, f32[40,128]{1,0:T(8,128)S(1)}, u32[]{:S(2)}, u32[]{:S(2)}) collective-permute-start(f32[40,128]{1,0:T(8,128)S(1)} %shard_map.71.iterate_ref), channel_id=1, source_target_pairs={{0,1},{1,0},{2,3},{3,2},{4,8},{5,9},{6,10},{7,11},{8,4},{9,5},{10,... | collective-permute-start | bytes 61448 | tf_op jit(solution)/shard_map/ppermute | solution.py:361
  22.0 3.3 %collective-permute-start.10 = (f32[40,128]{1,0:T(8,128)S(1)}, f32[40,128]{1,0:T(8,128)S(1)}, u32[]{:S(2)}, u32[]{:S(2)}) collective-permute-start(f32[40,128]{1,0:T(8,128)S(1)} %shard_map.73.iterate_ref), channel_id=1, source_target_pairs={{0,1},{1,0},{2,3},{3,2},{4,8},{5,9},{6,10},{7,11},{8,4},{9,5},{10,... | collective-permute-start | bytes 61448 | tf_op jit(solution)/shard_map/ppermute | solution.py:361
  22.2 3.0 %collective-permute-start.9 = (f32[40,128]{1,0:T(8,128)S(1)}, f32[40,128]{1,0:T(8,128)S(1)}, u32[]{:S(2)}, u32[]{:S(2)}) collective-permute-start(f32[40,128]{1,0:T(8,128)S(1)} %shard_map.73.iterate_ref), channel_id=1, source_target_pairs={{0,4},{1,5},{2,6},{3,7},{4,0},{5,1},{6,2},{7,3},{8,12},{9,13},{10,... | collective-permute-start | bytes 61448 | tf_op jit(solution)/shard_map/ppermute | solution.py:362
  23.1 5.2 %copy-start = (f32[15,3]{0,1:T(4,128)S(1)}, f32[15,3]{0,1:T(4,128)}, u32[]{:S(2)}) copy-start(f32[15,3]{0,1:T(4,128)} %param.8) | copy-start | bytes 544
  25.4 3.2 %collective-permute-start.11 = (f32[40,128]{1,0:T(8,128)S(1)}, f32[40,128]{1,0:T(8,128)S(1)}, u32[]{:S(2)}, u32[]{:S(2)}) collective-permute-start(f32[40,128]{1,0:T(8,128)S(1)} %shard_map.75.iterate_ref), channel_id=1, source_target_pairs={{0,4},{1,5},{2,6},{3,7},{4,0},{5,1},{6,2},{7,3},{8,12},{9,13},{10,... | collective-permute-start | bytes 61448 | tf_op jit(solution)/shard_map/ppermute | solution.py:362
  26.5 5.1 %collective-permute-start.12 = (f32[40,128]{1,0:T(8,128)S(1)}, f32[40,128]{1,0:T(8,128)S(1)}, u32[]{:S(2)}, u32[]{:S(2)}) collective-permute-start(f32[40,128]{1,0:T(8,128)S(1)} %shard_map.75.iterate_ref), channel_id=1, source_target_pairs={{4,8},{5,9},{6,10},{7,11},{8,4},{9,5},{10,6},{11,7},{12,16},{13,17... | collective-permute-start | bytes 61448 | tf_op jit(solution)/shard_map/ppermute | solution.py:361
